TPU v7x, 32 devices: a whole 2x2x4 slice. The times are simulated.
32 devices in a mesh: rep: 2 (over core), tab: 16 (over z, y, x).
Axes of the slice: x: 2, y: 2, z: 4, core: 2. Of those that a mesh axis runs over, the one named last changes fastest.
Arguments:
- grad_out: bfloat16 [8192, 16, 128], P(('rep', 'tab')), may hold values from -1.5 to 1.5
- indices: int32 [16, 8192], P('tab', 'rep'), may hold values from 0 to 1023
- projections: bfloat16 [16, 128, 128], P('tab'), may hold values from -0.75 to 0.75
- widths: int32 [16], replicated, may hold values from 16 to 128
- hot_ids: int32 [16, 32], P('tab'), may hold values from 0 to 1023, as said below
Outputs:
- cold_grad: float32 [2, 16, 1024, 128], P('rep', 'tab')
- hot_grad: float32 [16, 32, 128], P('tab', 'rep')
Inputs may be any that keep to these rules, and one draw needn't show every extreme that they name: `hot_ids`: the 32 hot rows of one table are distinct.
All inputs are finite; a program needn't handle non-finite values.
Results may differ from a plain program's by a relative error of at most 0.005.
Values may be sent and summed in bfloat16 or wider, within the bound.
No kernel may reach another device: no remote copies, remote signals or barrier semaphores. Data moves between devices by JAX's collectives and lax.ppermute only.
A program may use at most 128 MiB of HBM per device.

v0:
```python
import math

import jax
import jax.numpy as jnp
from jax import lax
from jax.sharding import PartitionSpec as P

ROWS = 1024


def swapped(block, axis, bit):
    count = lax.axis_size(axis)
    route = []
    for low in range(count):
        high = low | 1 << bit
        if high != low and high < count:
            route += [(low, high), (high, low)]
    return lax.ppermute(block, axis, route)


def block_sums(narrow_rows, lookups):
    total_len = narrow_rows.shape[0]
    block_len = math.gcd(total_len, 4096)
    turn_count = total_len // block_len
    positions = lax.broadcasted_iota(jnp.int32, (1, ROWS), 1)

    def add_block(block, totals):
        piece_rows = lax.dynamic_slice_in_dim(narrow_rows, block * block_len, block_len, 0)
        row_ids = lax.dynamic_slice_in_dim(lookups, block * block_len, block_len, 0)
        onehot = (row_ids[:, None] == positions).astype(jnp.bfloat16)
        return totals + lax.dot_general(
            onehot, piece_rows, (((0,), (0,)), ((), ())), preferred_element_type=jnp.float32
        )

    start_sums = jnp.zeros((ROWS, narrow_rows.shape[1]), jnp.float32)
    return lax.fori_loop(0, turn_count, add_block, start_sums)


def shards(grad_out, indices, projections, widths, hot_ids):
    tab_dev = projections.shape[0]
    base_width = projections.shape[2]
    columns = lax.broadcasted_iota(jnp.int32, (1, 1, base_width), 2)
    first_table = lax.axis_index("tab") * tab_dev
    own_widths = lax.dynamic_slice_in_dim(widths, first_table, tab_dev, 0)
    received = lax.all_to_all(grad_out, "tab", split_axis=1, concat_axis=0, tiled=True)
    full_proj = jnp.einsum(
        "bte,tej->tbj", received, projections, preferred_element_type=jnp.float32
    )
    narrow = jnp.where(columns < own_widths[:, None, None], full_proj, 0.0).astype(jnp.bfloat16)
    table_grads = [block_sums(narrow[0], indices[0])]
    row_grads = jnp.stack(table_grads)
    own_hot = jnp.take_along_axis(row_grads, hot_ids[:, :, None], axis=1)
    half_hot = hot_ids.shape[1] // 2
    replica = lax.axis_index("rep")
    kept_rows = lax.dynamic_slice_in_dim(own_hot, replica * half_hot, half_hot, 1)
    given_rows = lax.dynamic_slice_in_dim(own_hot, (1 - replica) * half_hot, half_hot, 1)
    partner = swapped(given_rows, "rep", 0)
    hot_grad = kept_rows + partner
    all_rows = lax.broadcasted_iota(jnp.int32, (1, 1, ROWS), 2)
    is_hot = jnp.any(hot_ids[:, :, None] == all_rows, axis=1)
    cold_grad = jnp.where(is_hot[:, :, None], jnp.float32(0.0), row_grads)
    return (cold_grad[None], hot_grad)


def solution(mesh):
    placed = (
        P(("rep", "tab"), None, None),
        P("tab", "rep"),
        P("tab", None, None),
        P(),
        P("tab", None),
    )
    return jax.shard_map(
        shards,
        mesh=mesh,
        in_specs=placed,
        out_specs=(P("rep", "tab", None, None), P("tab", "rep", None)),
        check_vma=False,
    )
```

profile of v0, /device:TPU:9, one launch (start us, length us, event | category | flops | bytes accessed | tf_op | source)
XLA Modules:
  0.0 44.1 jit_solution(15511810765626345854)
XLA Ops:
  0.6 0.0 copy-start
  0.6 2.5 %copy.8 = bf16[256,16,128]{2,0,1:T(8,128)(2,1)} copy(bf16[256,16,128]{2,1,0:T(8,128)(2,1)} %param.5) | data formatting | bytes 2097152 | tf_op args[0]
  3.1 0.0 copy-start.2
  3.1 0.0 copy-start.3
  3.1 0.0 copy-start.1
  3.1 6.8 %all-to-all-start = ((bf16[256,16,128]{2,0,1:T(8,128)(2,1)}), bf16[256,16,128]{2,0,1:T(8,128)(2,1)S(1)}, u32[]{:S(2)}, u32[]{:S(2)}) async-start(bf16[256,16,128]{2,0,1:T(8,128)(2,1)} %copy.8), calls=%async_computation | async-start | bytes 2097152 | tf_op jit(solution)/shard_map/all_to_all | solution.py:45
  9.9 0.0 copy-done.2
  9.9 0.6 %dynamic_slice.13 = s32[1]{0:T(128)} dynamic-slice(s32[16]{0:T(128)S(1)} %copy-done.2, s32[]{:T(128)S(6)} %select_n.55), dynamic_slice_sizes={1} | dynamic-slice | bytes 12 | tf_op jit(solution)/shard_map/dynamic_slice | solution.py:44
  10.5 0.6 %iota_compare_fusion.3 = pred[128]{0:T(512)(128)(4,1)S(1)} fusion(s32[]{:T(128)} %bitcast.2), kind=kLoop, calls=%fused_computation.20 | loop fusion | flops 128 | bytes 132 | tf_op jit(solution)/shard_map/lt | solution.py:49
  11.2 0.0 copy-done.3
  11.2 0.1 fusion.5
  11.3 23.0 %all-to-all-done = bf16[256,16,128]{2,0,1:T(8,128)(2,1)S(1)} async-done(((bf16[256,16,128]{2,0,1:T(8,128)(2,1)}), bf16[256,16,128]{2,0,1:T(8,128)(2,1)S(1)}, u32[]{:S(2)}, u32[]{:S(2)}) %all-to-all-start) | async-done | bytes 1048608 | tf_op jit(solution)/shard_map/all_to_all | solution.py:45
  34.3 0.0 copy-done
  34.3 0.0 copy-done.1
  34.3 5.1 %fusion = f32[1024,128]{1,0:T(8,128)S(1)} fusion(s32[4096]{0:T(1024)S(1)} %bitcast.23, bf16[4096,128]{1,0:T(8,128)(2,1)S(1)} %bitcast.22, pred[128]{0:T(512)(128)(4,1)S(1)} %iota_compare_fusion.3, bf16[1,128,128]{2,1,0:T(8,128)(2,1)S(1)} %copy-done), kind=kOutput, calls=%fused_computation.2 | convolution fusion | flops 1213202432 | bytes 1622144 | tf_op jit(solution)/shard_map/while/body/eval_jaxpr/dot_general | solution.py:31
  39.4 0.6 %gather_fusion = f32[32,128]{1,0:T(8,128)S(1)} fusion(f32[1024,128]{1,0:T(8,128)S(1)} %fusion, s32[1024]{0:T(1024)S(1)} %pad_clamp_fusion), kind=kCustom, calls=%fused_computation | custom fusion | bytes 32896 | tf_op jit(solution)/shard_map/jit(take_along_axis)/gather | solution.py:52
  40.0 0.1 bitcast_select_fusion
  40.1 2.4 %collective-permute-start = (f32[1,16,128]{2,1,0:T(8,128)S(1)}, f32[1,16,128]{2,1,0:T(8,128)S(1)}, u32[]{:S(2)}, u32[]{:S(2)}) collective-permute-start(f32[1,16,128]{2,1,0:T(8,128)S(1)} %constant_dynamic-slice_fusion), channel_id=1, source_target_pairs={{0,16},{16,0},{1,17},{17,1},{2,18},{18,2},{3,19},{19,3},{4,20},{20... | collective-permute-start | bytes 24584 | tf_op jit(solution)/shard_map/ppermute | solution.py:18
  42.5 1.0 %select_bitcast_fusion = f32[1,1,1024,128]{3,2,1,0:T(8,128)} fusion(f32[1024,128]{1,0:T(8,128)S(1)} %fusion, pred[1024]{0:T(1024)(128)(4,1)S(1)} %fusion.5), kind=kLoop, calls=%fused_computation.8 | loop fusion | flops 131072 | bytes 1049600 | tf_op jit(solution)/shard_map/broadcast_in_dim | solution.py:62
  43.5 0.0 collective-permute-done
  43.5 0.6 %dynamic-slice_add_fusion = f32[1,16,128]{2,1,0:T(8,128)} fusion(f32[1,16,128]{2,1,0:T(8,128)S(1)} %collective-permute-done, f32[1,32,128]{2,1,0:T(8,128)S(1)} %bitcast_select_fusion, s32[]{:T(128)S(6)} %select_n.61), kind=kLoop, calls=%fused_computation.13 | loop fusion | flops 2048 | bytes 24580 | tf_op jit(solution)/shard_map/add | solution.py:58
  (4 shorter events, 0.0 us)
Async XLA Ops:
  0.6 33.7 %copy-start = (bf16[1,128,128]{2,1,0:T(8,128)(2,1)S(1)}, bf16[1,128,128]{2,1,0:T(8,128)(2,1)}, u32[]{:S(2)}) copy-start(bf16[1,128,128]{2,1,0:T(8,128)(2,1)} %param.7) | copy-start | bytes 98308
  3.1 6.8 %copy-start.2 = (s32[16]{0:T(128)S(1)}, s32[16]{0:T(128)}, u32[]{:S(2)}) copy-start(s32[16]{0:T(128)} %param.8) | copy-start | bytes 196
  3.1 8.1 %copy-start.3 = (s32[1,32]{1,0:T(1,128)S(1)}, s32[1,32]{1,0:T(1,128)}, u32[]{:S(2)}) copy-start(s32[1,32]{1,0:T(1,128)} %param.9) | copy-start | bytes 388
  3.1 31.2 %copy-start.1 = (s32[1,4096]{1,0:T(1,128)S(1)}, s32[1,4096]{1,0:T(1,128)}, u32[]{:S(2)}) copy-start(s32[1,4096]{1,0:T(1,128)} %param.6) | copy-start | bytes 49156
  3.1 31.2 %all-to-all-start = ((bf16[256,16,128]{2,0,1:T(8,128)(2,1)}), bf16[256,16,128]{2,0,1:T(8,128)(2,1)S(1)}, u32[]{:S(2)}, u32[]{:S(2)}) async-start(bf16[256,16,128]{2,0,1:T(8,128)(2,1)} %copy.8), calls=%async_computation | async-start | bytes 2097152 | tf_op jit(solution)/shard_map/all_to_all | solution.py:45
  40.1 3.4 %collective-permute-start = (f32[1,16,128]{2,1,0:T(8,128)S(1)}, f32[1,16,128]{2,1,0:T(8,128)S(1)}, u32[]{:S(2)}, u32[]{:S(2)}) collective-permute-start(f32[1,16,128]{2,1,0:T(8,128)S(1)} %constant_dynamic-slice_fusion), channel_id=1, source_target_pairs={{0,16},{16,0},{1,17},{17,1},{2,18},{18,2},{3,19},{19,3},{4,20},{20... | collective-permute-start | bytes 24584 | tf_op jit(solution)/shard_map/ppermute | solution.py:18
where the time goes:
time: 44.4 us; the launch traced here: 44.1 us
  waiting for transfers between devices  23 us (52%)
  starting transfers between devices  9.21 us (21%)
  matrix products  5.13 us (12%)
  local copies, waits for them, and re-layouts  3.65 us (8%)
  other arithmetic  2.44 us (5%)
  between operations  0.69 us (2%)
    all_to_all x1, waiting for transfers between devices, shards(): lax.all_to_all(grad_out, 'tab', split_axis=1, concat_axis=0, tiled=True)  23 us
    all_to_all x1, starting transfers between devices, shards(): lax.all_to_all(grad_out, 'tab', split_axis=1, concat_axis=0, tiled=True)  6.8 us
    dot_general x1, matrix products, add_block(): lax.dot_general(onehot, piece_rows, (((0,), (0,)), ((), ())), preferred_e...  5.13 us
    unnamed x9, local copies, waits for them, and re-layouts  2.49 us
    ppermute x1, starting transfers between devices, swapped(): return lax.ppermute(block, axis, route)  2.41 us
    broadcast_in_dim x1, other arithmetic, shards(): return (cold_grad[None], hot_grad)  1 us
  transfers between devices with their start and end apart: 2, of which 1 were waited for; matrix products, arithmetic and copies ran while one was open for 5% of the time, Pallas kernels for 0%

commit v1 on v0

v1 whole, which is shorter than its diff:
```python
import math

import jax
import jax.numpy as jnp
from jax import lax
from jax.experimental import pallas as pl
from jax.experimental.pallas import tpu as pltpu
from jax.sharding import PartitionSpec as P


ROWS = 1024
LOW = ROWS // 2
SUB = 8
STEP = 32
LANES = 128
MOST_PEERS = 16
VM = pl.BlockSpec(memory_space=pltpu.VMEM)
SM = pl.BlockSpec(memory_space=pltpu.SMEM)
HB = pl.BlockSpec(memory_space=pltpu.HBM)


def cost(flops, nbytes):
    return pl.CostEstimate(flops=int(flops), bytes_accessed=int(nbytes), transcendentals=0)


def room(mib):
    return pltpu.CompilerParams(vmem_limit_bytes=mib << 20)


def spread(values, group):
    take = lax.broadcasted_iota(jnp.int32, (SUB * STEP, SUB * STEP), 1)
    place = lax.broadcasted_iota(jnp.int32, (SUB * STEP, SUB * STEP), 0)
    swap = (take == (place % STEP) * SUB + ((place // STEP) ^ group)).astype(jnp.float32).astype(jnp.bfloat16)
    return [
        jnp.dot(swap, rows.reshape(SUB * STEP, rows.shape[-1]), preferred_element_type=jnp.float32).astype(jnp.bfloat16)
        for rows in values
    ]


def prep_body(grads, lookups, hot, notes, *refs):
    outs, (held, listed, sems, note_sems) = refs[:-4], refs[-4:]
    spd = grads.shape[0]
    me = lax.axis_index("tab")
    chunks = sems.shape[0]
    size = spd // chunks
    length = lookups.shape[1]
    moves = []
    for chunk in range(chunks):
        where = pl.ds(chunk * size, size)
        moves.append(pltpu.make_async_copy(grads.at[where], held.at[where], sems.at[chunk]))
        moves[-1].start()
    hot_move = pltpu.make_async_copy(hot, listed, note_sems.at[0])
    hot_move.start()
    note_move = pltpu.make_async_copy(lookups, notes.at[:, pl.ds(0, length)], note_sems.at[1])
    note_move.start()
    notes[:, pl.ds(length, LANES)] = jnp.full((1, LANES), -1, jnp.int32)
    relay = outs[-1]
    for chunk in range(chunks):
        lows = range(chunk * size, (chunk + 1) * size, STEP)
        moves[chunk].wait()
        for group in range(2):
            which = (me // SUB) ^ (1 - group)
            for low, turned in zip(lows, spread([held[pl.ds(low, STEP), which] for low in lows], me % SUB)):
                for at in range(SUB):
                    rows = turned[at * STEP:(at + 1) * STEP]
                    if group == 0:
                        outs[at][pl.ds(low, STEP), :] = rows
                    elif at < SUB // 2:
                        outs[at][pl.ds(spd + low, STEP), :] = rows
                    else:
                        relay[pl.ds((at - SUB // 2) * spd + low, STEP), :] = rows
    hot_move.wait()
    notes[:, pl.ds(length, hot.shape[1])] = listed[...]
    note_move.wait()


def prep(grads, lookups, hot):
    spd, _, _, width = grads.shape

    def block(parts):
        return jax.ShapeDtypeStruct((parts * spd, width), jnp.bfloat16)

    half = SUB // 2
    kept = [pltpu.with_memory_space_constraint(x, pltpu.HBM) for x in (grads, lookups, hot)]
    return pl.pallas_call(
        prep_body,
        out_shape=(jax.ShapeDtypeStruct((1, lookups.shape[1] + LANES), jnp.int32),)
        + (block(2),) * half
        + (block(1),) * half
        + (block(half),),
        in_specs=[HB] * 3,
        out_specs=(VM,) * (SUB + 2),
        scratch_shapes=[
            pltpu.VMEM((spd, 2, SUB, width), jnp.bfloat16),
            pltpu.VMEM((1, hot.shape[1]), jnp.int32),
            pltpu.SemaphoreType.DMA((4,)),
            pltpu.SemaphoreType.DMA((2,)),
        ],
        compiler_params=room(5),
        cost_estimate=cost(2 * SUB * spd * width * 512, 2 * SUB * spd * width * 4),
        name="prep",
    )(*kept)


def match_body(notes, low_match, high_side, hot_match):
    total = low_match.shape[1]
    size = LANES
    half = lax.axis_index("tab") // (lax.axis_size("tab") // 2)
    quarter = LOW // 2
    lows = lax.broadcasted_iota(jnp.int32, (quarter, size), 0).astype(jnp.float32).astype(jnp.bfloat16)
    one, zero = jnp.bfloat16(1), jnp.bfloat16(0)
    hot = notes[:, pl.ds(notes.shape[1] - LANES, LANES)].astype(jnp.float32)
    hot = jnp.broadcast_to(hot, (LANES, LANES)).T[:hot_match.shape[0]]
    for start in range(0, total, size):
        ids = notes[:, pl.ds(pl.multiple_of(half * total + start, size), size)]
        same = jnp.where(hot == ids.astype(jnp.float32), 1.0, 0.0)
        hot_match[:, pl.ds(start, size)] = same.astype(jnp.bfloat16)
        cold = (1.0 - jnp.sum(same, axis=0, keepdims=True)).astype(jnp.bfloat16)
        low = (ids % quarter).astype(jnp.float32).astype(jnp.bfloat16)
        middle = ((ids // quarter) % 2).astype(jnp.float32).astype(jnp.bfloat16)
        match = jnp.where(low == lows, one, zero)
        for top in range(2):
            keep = jnp.where(middle == jnp.bfloat16(top), cold, jnp.zeros_like(cold))
            low_match[pl.ds(top * quarter, quarter), pl.ds(start, size)] = match * keep
        high = (ids // LOW).astype(jnp.float32)
        high_side[pl.ds(start, size), :] = jnp.broadcast_to(high, (LANES, size)).T.astype(jnp.bfloat16)


def match(notes, total, hots):
    return pl.pallas_call(
        match_body,
        out_shape=(
            jax.ShapeDtypeStruct((LOW, total), jnp.bfloat16),
            jax.ShapeDtypeStruct((total, LANES), jnp.bfloat16),
            jax.ShapeDtypeStruct((hots, total), jnp.bfloat16),
        ),
        in_specs=[VM],
        out_specs=(VM,) * 3,
        compiler_params=room(8),
        cost_estimate=cost(LOW * total * 400, LOW * total * 2),
    )(notes)


def gather(spd, pieces, high_side, both, rows):
    width = rows.shape[1]
    near = lax.axis_size("tab") // 2
    me = lax.axis_index("tab") % near
    for shift, chunk, first in pieces:
        where = pl.ds(pl.multiple_of((me ^ shift) * spd, spd), spd)
        piece = chunk[pl.ds(first, spd), :]
        upper = piece * high_side[where, :]
        both[where, :width] = piece - upper
        both[where, width:] = upper
        rows[where, :] = piece


def split(value):
    half = value.shape[0] // 2
    lower, upper = value[:half], value[half:]
    first = lax.axis_index("rep") == 0
    return jnp.where(first, lower, upper), jnp.where(first, upper, lower)


def other_body(low_match, high_side, hot_match, *refs):
    chunks, (out, given, both, rows) = refs[:-4], refs[-4:]
    spd = rows.shape[0] // len(chunks)
    gather(spd, [(at, chunk, 0) for at, chunk in enumerate(chunks)], high_side, both, rows)
    width = rows.shape[1]
    hot = jnp.dot(hot_match[...], rows[...], preferred_element_type=jnp.float32)
    kept, given[...] = split(hot)
    part = jnp.dot(low_match[...], both[...], preferred_element_type=jnp.float32)
    for top in range(2):
        out[pl.ds(top * LOW, LOW), :] = part[:, top * width:(top + 1) * width].astype(jnp.bfloat16)
    out[pl.ds(ROWS, kept.shape[0]), :] = kept.astype(jnp.bfloat16)


def scratch(matched, width):
    total = matched[1].shape[0]
    return [pltpu.VMEM((total, 2 * width), jnp.bfloat16), pltpu.VMEM((total, width), jnp.bfloat16)]


def other_sums(chunks, matched):
    width = chunks[0].shape[1]
    total, half = matched[1].shape[0], matched[2].shape[0] // 2
    return pl.pallas_call(
        other_body,
        out_shape=(
            jax.ShapeDtypeStruct((ROWS + half, width), jnp.bfloat16),
            jax.ShapeDtypeStruct((half, width), jnp.float32),
        ),
        in_specs=[VM] * (3 + len(chunks)),
        out_specs=(VM, VM),
        scratch_shapes=scratch(matched, width),
        compiler_params=room(8),
        cost_estimate=cost(2 * total * width * ROWS, total * width * 2),
        name="other_sums",
    )(*matched, *chunks)


def project(values, matrix):
    high = values.astype(jnp.bfloat16)
    low = (values - high.astype(jnp.float32)).astype(jnp.bfloat16)
    return jnp.dot(high, matrix, preferred_element_type=jnp.float32) + jnp.dot(
        low, matrix, preferred_element_type=jnp.float32
    )


def partial_sums(spd, pieces, low_match, high_side, hot_match):
    near = lax.axis_size("tab") // 2
    me = lax.axis_index("tab") % near
    sides, lows, hots, rows = [], [], [], []
    for shift, chunk, first in pieces:
        where = pl.ds(pl.multiple_of((me ^ shift) * spd, spd), spd)
        piece = chunk[pl.ds(first, spd), :]
        upper = piece * high_side[where, :]
        sides.append(jnp.concatenate([piece - upper, upper], axis=1))
        lows.append(low_match[:, where])
        hots.append(hot_match[:, where])
        rows.append(piece)
    both = jnp.dot(jnp.concatenate(lows, axis=1), jnp.concatenate(sides, axis=0), preferred_element_type=jnp.float32)
    hot = jnp.dot(jnp.concatenate(hots, axis=1), jnp.concatenate(rows, axis=0), preferred_element_type=jnp.float32)
    return both, hot


def early_body(low_match, high_side, hot_match, own, one, two, three, relayed, total, hot):
    spd = own.shape[0] // 2
    pieces = [(0, own, spd), (1, one, spd), (2, two, spd), (3, three, spd), (4, relayed, 0)]
    total[...], hot[...] = partial_sums(spd, pieces, low_match, high_side, hot_match)


def early_sums(matched, chunks):
    width = chunks[0].shape[1]
    count = matched[1].shape[0]
    return pl.pallas_call(
        early_body,
        out_shape=(
            jax.ShapeDtypeStruct((LOW, 2 * width), jnp.float32),
            jax.ShapeDtypeStruct((matched[2].shape[0], width), jnp.float32),
        ),
        in_specs=[VM] * 8,
        out_specs=(VM, VM),
        compiler_params=room(8),
        cost_estimate=cost(count * width * ROWS, count * width * 2),
        name="early_sums",
    )(*matched, *chunks)


def own_body(widths, proj, low_match, high_side, hot_match, total, hot, *refs):
    chunks, (done, matrix, kept, given) = refs[:-4], refs[-4:]
    spd, width = chunks[0].shape
    columns = lax.broadcasted_iota(jnp.int32, proj.shape, 1)
    limit = widths[lax.axis_index("tab")]
    matrix[...] = jnp.where(columns < limit, proj[...].astype(jnp.float32), 0.0).astype(jnp.bfloat16)
    pieces = [(5 + at, chunk, 0) for at, chunk in enumerate(chunks)]
    both, more = partial_sums(spd, pieces, low_match, high_side, hot_match)
    kept[...], given[...] = split(hot[...] + more)
    both += total[...]
    for top in range(2):
        done[pl.ds(top * LOW, LOW), :] = project(both[:, top * width:(top + 1) * width], matrix[...])


def own_sums(matched, early, chunks, proj, widths):
    width = chunks[0].shape[1]
    count, half = matched[1].shape[0], matched[2].shape[0] // 2
    part = jax.ShapeDtypeStruct((half, width), jnp.float32)
    return pl.pallas_call(
        own_body,
        out_shape=(
            jax.ShapeDtypeStruct((ROWS, width), jnp.float32),
            jax.ShapeDtypeStruct((width, width), jnp.bfloat16),
            part,
            part,
        ),
        in_specs=[SM] + [VM] * (6 + len(chunks)),
        out_specs=(VM,) * 4,
        compiler_params=room(8),
        cost_estimate=cost(count * width * ROWS, count * width * 2),
        name="own_sums",
    )(widths, proj, *matched, *early, *chunks)


def cut_body(block, *outs):
    spd = outs[0].shape[0]
    for at, out in enumerate(outs):
        out[...] = block[pl.ds((at + 1) * spd, spd), :]


def cut(block, parts):
    spd, width = block.shape[0] // parts, block.shape[1]
    return pl.pallas_call(
        cut_body,
        out_shape=(jax.ShapeDtypeStruct((spd, width), block.dtype),) * (parts - 1),
        in_specs=[VM],
        out_specs=(VM,) * (parts - 1),
        compiler_params=room(2),
        cost_estimate=cost(block.size * 20, block.size * 4),
        name="cut",
    )(block)


PIECES = 4


def last_body(done, matrix, kept, far, same_chip, far_chip, cold, hot, held, sems):
    size = ROWS // PIECES
    table = matrix[...]
    moves = []
    for piece in range(PIECES):
        where = pl.ds(piece * size, size)
        held[where, :] = done[where, :] + jnp.dot(far[where, :], table, preferred_element_type=jnp.float32)
        moves.append(pltpu.make_async_copy(held.at[where], cold.at[where], sems.at[piece]))
        moves[-1].start()
    hot_far = far[pl.ds(ROWS, hot.shape[0]), :].astype(jnp.float32)
    hot[...] = project(kept[...] + hot_far + same_chip[...] + far_chip[...], table)
    for one in moves:
        one.wait()


def last(done, matrix, kept, far, same_chip, far_chip):
    half, width = same_chip.shape
    return pl.pallas_call(
        last_body,
        out_shape=(
            jax.ShapeDtypeStruct((ROWS, width), jnp.float32),
            jax.ShapeDtypeStruct((half, width), jnp.float32),
        ),
        in_specs=[VM] * 6,
        out_specs=(HB, VM),
        scratch_shapes=[
            pltpu.VMEM((ROWS, width), jnp.float32),
            pltpu.SemaphoreType.DMA((PIECES,)),
        ],
        compiler_params=room(4),
        cost_estimate=cost(4 * ROWS * width * width, ROWS * width * 10),
        name="last",
    )(done, matrix, kept, far, same_chip, far_chip)


def swap_reps(block):
    reps = lax.axis_size("rep")
    return lax.ppermute(block, "rep", [(r, r ^ 1) for r in range(reps)])


FIRST = (7, 6, 5, 4, 3, 2, 1)
PLANE = (1, 2, 3)


def shards(grad_out, indices, projections, widths, hot_ids):
    count, reps = lax.axis_size("tab"), lax.axis_size("rep")
    spd, tables, width = grad_out.shape
    half_len = count // 2 * spd
    hots = hot_ids.shape[1]
    grads = grad_out.reshape(spd, tables // SUB, SUB, width)

    def send(block, shift):
        return lax.ppermute(block, "tab", [(i, i ^ shift) for i in range(count)])

    notes, *blocks, relay = prep(grads, indices, hot_ids)
    got = {0: blocks[0]}
    for shift in FIRST:
        got[shift] = send(blocks[shift], shift)
    far_notes = send(notes, SUB)
    relayed = send(relay, SUB // 2)
    far_matched = match(far_notes, half_len, hots)
    partial, far_given = other_sums([got[shift] for shift in range(SUB)], far_matched)
    far = send(partial, SUB)
    pieces = cut(relayed, SUB // 2)
    second = [send(pieces[shift - 1], shift) for shift in PLANE]
    far_chip = lax.ppermute(
        far_given,
        ("rep", "tab"),
        [(r * count + i, (r ^ 1) * count + (i ^ SUB)) for r in range(reps) for i in range(count)],
    )
    own_matched = match(notes, half_len, hots)
    early = early_sums(own_matched, [got[0], got[1], got[2], got[3], relayed])
    done, matrix, kept, given = own_sums(own_matched, early, second, projections[0], widths)
    same_chip = swap_reps(given)
    cold, hot = last(done, matrix, kept, far, same_chip, far_chip)
    return cold[None, None], hot[None]


def block_sums(narrow_rows, lookups):
    total_len = narrow_rows.shape[0]
    block_len = math.gcd(total_len, 4096)
    positions = lax.broadcasted_iota(jnp.int32, (1, ROWS), 1)

    def add_block(block, totals):
        piece_rows = lax.dynamic_slice_in_dim(narrow_rows, block * block_len, block_len, 0)
        row_ids = lax.dynamic_slice_in_dim(lookups, block * block_len, block_len, 0)
        onehot = (row_ids[:, None] == positions).astype(jnp.bfloat16)
        return totals + lax.dot_general(
            onehot, piece_rows, (((0,), (0,)), ((), ())), preferred_element_type=jnp.float32
        )

    start_sums = jnp.zeros((ROWS, narrow_rows.shape[1]), jnp.float32)
    return lax.fori_loop(0, total_len // block_len, add_block, start_sums)


def many_shards(grad_out, indices, projections, widths, hot_ids):
    columns = lax.broadcasted_iota(jnp.int32, (1, projections.shape[2]), 1)
    limit = lax.dynamic_slice_in_dim(widths, lax.axis_index("tab"), 1, 0)
    received = lax.all_to_all(grad_out, "tab", split_axis=1, concat_axis=0, tiled=True)
    full_proj = jnp.einsum("be,ej->bj", received[:, 0], projections[0], preferred_element_type=jnp.float32)
    narrow = jnp.where(columns < limit[:, None], full_proj, 0.0).astype(jnp.bfloat16)
    row_grads = block_sums(narrow, indices[0])
    own_hot = row_grads[hot_ids[0]]
    half_hot = own_hot.shape[0] // 2
    replica = lax.axis_index("rep")
    kept_rows = lax.dynamic_slice_in_dim(own_hot, replica * half_hot, half_hot, 0)
    given_rows = lax.dynamic_slice_in_dim(own_hot, (1 - replica) * half_hot, half_hot, 0)
    hot_grad = kept_rows + swap_reps(given_rows)
    all_rows = lax.broadcasted_iota(jnp.int32, (ROWS, 1), 0)
    is_hot = jnp.any(hot_ids == all_rows, axis=1)
    cold_grad = jnp.where(is_hot[:, None], jnp.float32(0.0), row_grads)
    return cold_grad[None, None], hot_grad[None]


def solution(mesh):
    placed = (
        P(("rep", "tab"), None, None),
        P("tab", "rep"),
        P("tab", None, None),
        P(),
        P("tab", None),
    )
    few = mesh.shape["tab"] <= MOST_PEERS
    return jax.shard_map(
        shards if few else many_shards,
        mesh=mesh,
        in_specs=placed,
        out_specs=(P("rep", "tab", None, None), P("tab", "rep", None)),
        check_vma=False,
    )
```

time: 44.4 us -> 38.9 us (0.88)
  the two profiles are of different devices: /device:TPU:9 before, /device:TPU:0 now
where the time goes in v1:
time: 38.9 us; the launch traced here: 38.8 us
  starting transfers between devices  18.7 us (48%)
  waiting for transfers between devices  10.7 us (28%)
  Pallas kernels  8.61 us (22%)
  between operations  0.75 us (2%)
    ppermute x13, starting transfers between devices, send(): return lax.ppermute(block, 'tab', [(i, i ^ shift) for i in range(count)])  18.6 us
    ppermute x13, waiting for transfers between devices, send(): return lax.ppermute(block, 'tab', [(i, i ^ shift) for i in range(count)])  9.56 us
    pallas_call x1, Pallas kernels, prep(): pl.pallas_call(prep_body, out_shape=(jax.ShapeDtypeStruct((1, lookups.sha...  2.16 us
    pallas_call x2, Pallas kernels, match(): pl.pallas_call(match_body, out_shape=(jax.ShapeDtypeStruct((LOW, total),...  1.83 us
    pallas_call x1, Pallas kernels, last(): pl.pallas_call(last_body, out_shape=(jax.ShapeDtypeStruct((ROWS, width),...  1.59 us
    pallas_call x1, Pallas kernels, own_sums(): pl.pallas_call(own_body, out_shape=(jax.ShapeDtypeStruct((ROWS, width), j...  1.39 us
    ppermute x1, waiting for transfers between devices, swap_reps(): return lax.ppermute(block, 'rep', [(r, r ^ 1) for r in range(reps)])  1.15 us
    pallas_call x1, Pallas kernels, other_sums(): pl.pallas_call(other_body, out_shape=(jax.ShapeDtypeStruct((ROWS + half,...  1.06 us
  transfers between devices with their start and end apart: 15, of which 6 were waited for; matrix products, arithmetic and copies ran while one was open for 0% of the time, Pallas kernels for 13%

profile of v1, /device:TPU:0, one launch (start us, length us, event | category | flops | bytes accessed | tf_op | source)
XLA Modules:
  0.0 38.8 jit_solution(17471900093442282955)
XLA Ops:
  0.6 2.2 %prep.1 = (s32[1,4224]{1,0:T(1,128)S(1)}, bf16[512,128]{1,0:T(8,128)(2,1)S(1)}, bf16[512,128]{1,0:T(8,128)(2,1)S(1)}, bf16[512,128]{1,0:T(8,128)(2,1)S(1)}, bf16...) custom-call(bf16[256,2,8,128]{3,2,1,0:T(8,128)(2,1)} %bitcast.5, ...), custom_call_target="tpu_custom_call" | custom-call | flops 268435456 | bytes 2097152 | tf_op jit(solution)/shard_map/prep/pallas_call | solution.py:85
  2.8 4.1 %collective-permute-start.10 = (bf16[256,128]{1,0:T(8,128)(2,1)S(1)}, bf16[256,128]{1,0:T(8,128)(2,1)S(1)}, u32[]{:S(2)}, u32[]{:S(2)}) collective-permute-start(bf16[256,128]{1,0:T(8,128)(2,1)S(1)} %get-tuple-element.53), channel_id=1, source_target_pairs={{0,6},{1,7},{2,4},{3,5},{4,2},{5,3},{6,0},{7,1},{8,14},{9,15},{10,... | collective-permute-start | bytes 196616 | tf_op jit(solution)/shard_map/ppermute | solution.py:356
  6.9 2.6 %collective-permute-start.7 = (s32[1,4224]{1,0:T(1,128)S(1)}, s32[1,4224]{1,0:T(1,128)S(1)}, u32[]{:S(2)}, u32[]{:S(2)}) collective-permute-start(s32[1,4224]{1,0:T(1,128)S(1)} %get-tuple-element.31.notes), channel_id=1, source_target_pairs={{0,8},{1,9},{2,10},{3,11},{4,12},{5,13},{6,14},{7,15},{8,0},{9,1},... | collective-permute-start | bytes 50696 | tf_op jit(solution)/shard_map/ppermute | solution.py:356
  9.5 1.5 %collective-permute-start = (bf16[512,128]{1,0:T(8,128)(2,1)S(1)}, bf16[512,128]{1,0:T(8,128)(2,1)S(1)}, u32[]{:S(2)}, u32[]{:S(2)}) collective-permute-start(bf16[512,128]{1,0:T(8,128)(2,1)S(1)} %get-tuple-element.36), channel_id=1, source_target_pairs={{0,1},{1,0},{2,3},{3,2},{4,5},{5,4},{6,7},{7,6},{8,9},{9,8},{10,11... | collective-permute-start | bytes 393224 | tf_op jit(solution)/shard_map/ppermute | solution.py:356
  11.0 0.4 collective-permute-start.11
  11.3 1.5 %collective-permute-start.1 = (bf16[512,128]{1,0:T(8,128)(2,1)S(1)}, bf16[512,128]{1,0:T(8,128)(2,1)S(1)}, u32[]{:S(2)}, u32[]{:S(2)}) collective-permute-start(bf16[512,128]{1,0:T(8,128)(2,1)S(1)} %get-tuple-element.37), channel_id=1, source_target_pairs={{0,2},{1,3},{2,0},{3,1},{4,6},{5,7},{6,4},{7,5},{8,10},{9,11},{10,... | collective-permute-start | bytes 393224 | tf_op jit(solution)/shard_map/ppermute | solution.py:356
  12.8 1.4 %collective-permute-start.2 = (bf16[512,128]{1,0:T(8,128)(2,1)S(1)}, bf16[512,128]{1,0:T(8,128)(2,1)S(1)}, u32[]{:S(2)}, u32[]{:S(2)}) collective-permute-start(bf16[512,128]{1,0:T(8,128)(2,1)S(1)} %get-tuple-element.38), channel_id=1, source_target_pairs={{0,3},{1,2},{2,1},{3,0},{4,7},{5,6},{6,5},{7,4},{8,11},{9,10},{10,... | collective-permute-start | bytes 393224 | tf_op jit(solution)/shard_map/ppermute | solution.py:356
  14.3 1.6 %collective-permute-start.8 = (bf16[256,128]{1,0:T(8,128)(2,1)S(1)}, bf16[256,128]{1,0:T(8,128)(2,1)S(1)}, u32[]{:S(2)}, u32[]{:S(2)}) collective-permute-start(bf16[256,128]{1,0:T(8,128)(2,1)S(1)} %get-tuple-element.51), channel_id=1, source_target_pairs={{0,4},{1,5},{2,6},{3,7},{4,0},{5,1},{6,2},{7,3},{8,12},{9,13},{10,... | collective-permute-start | bytes 196616 | tf_op jit(solution)/shard_map/ppermute | solution.py:356
  15.9 1.5 %collective-permute-done.11.refs_7_ = bf16[256,128]{1,0:T(8,128)(2,1)S(1)} collective-permute-done((bf16[256,128]{1,0:T(8,128)(2,1)S(1)}, bf16[256,128]{1,0:T(8,128)(2,1)S(1)}, u32[]{:S(2)}, u32[]{:S(2)}) %collective-permute-start.11) | collective-permute-done | bytes 65568 | tf_op jit(solution)/shard_map/ppermute | solution.py:356
  17.6 1.7 %collective-permute-done.8.refs_4_ = bf16[256,128]{1,0:T(8,128)(2,1)S(1)} collective-permute-done((bf16[256,128]{1,0:T(8,128)(2,1)S(1)}, bf16[256,128]{1,0:T(8,128)(2,1)S(1)}, u32[]{:S(2)}, u32[]{:S(2)}) %collective-permute-start.8) | collective-permute-done | bytes 65568 | tf_op jit(solution)/shard_map/ppermute | solution.py:356
  19.2 1.0 %collective-permute-start.3 = (bf16[1024,128]{1,0:T(8,128)(2,1)S(1)}, bf16[1024,128]{1,0:T(8,128)(2,1)S(1)}, u32[]{:S(2)}, u32[]{:S(2)}) collective-permute-start(bf16[1024,128]{1,0:T(8,128)(2,1)S(1)} %get-tuple-element.39), channel_id=1, source_target_pairs={{0,4},{1,5},{2,6},{3,7},{4,0},{5,1},{6,2},{7,3},{8,12},{9,13},{10,... | collective-permute-start | bytes 786440 | tf_op jit(solution)/shard_map/ppermute | solution.py:356
  20.2 0.9 %shard_map.69 = (bf16[512,2048]{1,0:T(8,128)(2,1)S(1)}, bf16[2048,128]{1,0:T(8,128)(2,1)S(1)}, bf16[32,2048]{1,0:T(8,128)(2,1)S(1)}) custom-call(s32[1,4224]{1,0:T(1,128)S(1)} %collective-permute-done.7.notes), custom_call_target="tpu_custom_call" | custom-call | flops 419430400 | bytes 2097152 | tf_op jit(solution)/shard_map/pallas_call | solution.py:130
  21.1 1.6 %collective-permute-done.9.refs_5_ = bf16[256,128]{1,0:T(8,128)(2,1)S(1)} collective-permute-done((bf16[256,128]{1,0:T(8,128)(2,1)S(1)}, bf16[256,128]{1,0:T(8,128)(2,1)S(1)}, u32[]{:S(2)}, u32[]{:S(2)}) %collective-permute-start.9) | collective-permute-done | bytes 65568 | tf_op jit(solution)/shard_map/ppermute | solution.py:356
  22.7 1.1 %other_sums.1 = (bf16[1040,128]{1,0:T(8,128)(2,1)S(1)}, f32[16,128]{1,0:T(8,128)S(1)}) custom-call(bf16[512,2048]{1,0:T(8,128)(2,1)S(1)} %get-tuple-element.48.low_match, bf16[2048,128]{1,0:T(8,128)(2,1)S(1)} %get-tuple-element.49.high_side, bf16[32,2048]{1,0:T(8,128)(2,1)S(1)} %get-tuple-element.50.hot_match, ...), custom_call_target="tpu_custom_call" | custom-call | flops 536870912 | bytes 524288 | tf_op jit(solution)/shard_map/other_sums/pallas_call | solution.py:185
  23.8 0.8 %collective-permute-start.12 = (bf16[1040,128]{1,0:T(8,128)(2,1)S(1)}, bf16[1040,128]{1,0:T(8,128)(2,1)S(1)}, u32[]{:S(2)}, u32[]{:S(2)}) collective-permute-start(bf16[1040,128]{1,0:T(8,128)(2,1)S(1)} %get-tuple-element.55), channel_id=1, source_target_pairs={{0,8},{1,9},{2,10},{3,11},{4,12},{5,13},{6,14},{7,15},{8,0},{9,1},... | collective-permute-start | bytes 798728 | tf_op jit(solution)/shard_map/ppermute | solution.py:356
  24.6 2.7 %collective-permute-done.3.relayed.block = bf16[1024,128]{1,0:T(8,128)(2,1)S(1)} collective-permute-done((bf16[1024,128]{1,0:T(8,128)(2,1)S(1)}, bf16[1024,128]{1,0:T(8,128)(2,1)S(1)}, u32[]{:S(2)}, u32[]{:S(2)}) %collective-permute-start.3) | collective-permute-done | bytes 262176 | tf_op jit(solution)/shard_map/ppermute | solution.py:356
  27.6 1.7 %collective-permute-start.5 = (bf16[256,128]{1,0:T(8,128)(2,1)S(1)}, bf16[256,128]{1,0:T(8,128)(2,1)S(1)}, u32[]{:S(2)}, u32[]{:S(2)}) collective-permute-start(bf16[256,128]{1,0:T(8,128)(2,1)S(1)} %get-tuple-element.43), channel_id=1, source_target_pairs={{0,2},{1,3},{2,0},{3,1},{4,6},{5,7},{6,4},{7,5},{8,10},{9,11},{10,... | collective-permute-start | bytes 196616 | tf_op jit(solution)/shard_map/ppermute | solution.py:356
  29.4 1.5 %collective-permute-start.6 = (bf16[256,128]{1,0:T(8,128)(2,1)S(1)}, bf16[256,128]{1,0:T(8,128)(2,1)S(1)}, u32[]{:S(2)}, u32[]{:S(2)}) collective-permute-start(bf16[256,128]{1,0:T(8,128)(2,1)S(1)} %get-tuple-element.44), channel_id=1, source_target_pairs={{0,3},{1,2},{2,1},{3,0},{4,7},{5,6},{6,5},{7,4},{8,11},{9,10},{10,... | collective-permute-start | bytes 196616 | tf_op jit(solution)/shard_map/ppermute | solution.py:356
  30.9 0.9 %shard_map.68 = (bf16[512,2048]{1,0:T(8,128)(2,1)S(1)}, bf16[2048,128]{1,0:T(8,128)(2,1)S(1)}, bf16[32,2048]{1,0:T(8,128)(2,1)S(1)}) custom-call(s32[1,4224]{1,0:T(1,128)S(1)} %get-tuple-element.31.notes), custom_call_target="tpu_custom_call" | custom-call | flops 419430400 | bytes 2097152 | tf_op jit(solution)/shard_map/pallas_call | solution.py:130
  31.9 0.6 %early_sums.1 = (f32[512,256]{1,0:T(8,128)S(1)}, f32[32,128]{1,0:T(8,128)S(1)}) custom-call(bf16[512,2048]{1,0:T(8,128)(2,1)S(1)} %get-tuple-element.32.low_match, bf16[2048,128]{1,0:T(8,128)(2,1)S(1)} %get-tuple-element.33.high_side, bf16[32,2048]{1,0:T(8,128)(2,1)S(1)} %get-tuple-element.34.hot_match, bf16[512,128]{1,0:T(8,128)(2,1)S(1)} %get-tuple-element.35.own.refs_0_, ...), custom_call_target="tpu_custom_call" | custom-call | flops 268435456 | bytes 524288 | tf_op jit(solution)/shard_map/early_sums/pallas_call | solution.py:234
  32.5 2.0 %collective-permute-done.6.refs_2_ = bf16[256,128]{1,0:T(8,128)(2,1)S(1)} collective-permute-done((bf16[256,128]{1,0:T(8,128)(2,1)S(1)}, bf16[256,128]{1,0:T(8,128)(2,1)S(1)}, u32[]{:S(2)}, u32[]{:S(2)}) %collective-permute-start.6) | collective-permute-done | bytes 65568 | tf_op jit(solution)/shard_map/ppermute | solution.py:356
  34.5 1.4 %own_sums.1 = (f32[1024,128]{1,0:T(8,128)S(1)}, bf16[128,128]{1,0:T(8,128)(2,1)S(1)}, f32[16,128]{1,0:T(8,128)S(1)}, f32[16,128]{1,0:T(8,128)S(1)}) custom-call(s32[16]{0:T(128)S(1)} %copy-done.1, bf16[128,128]{1,0:T(8,128)(2,1)S(1)} %bitcast.4, bf16[512,2048]{1,0:T(8,128)(2,1)S(1)} %get-tuple-element.32.low_match, ...), custom_call_target="tpu_custom_call" | custom-call | flops 268435456 | bytes 524288 | tf_op jit(solution)/shard_map/own_sums/pallas_call | solution.py:266
  36.0 1.1 %collective-permute-done.13.same_chip = f32[16,128]{1,0:T(8,128)S(1)} collective-permute-done((f32[16,128]{1,0:T(8,128)S(1)}, f32[16,128]{1,0:T(8,128)S(1)}, u32[]{:S(2)}, u32[]{:S(2)}) %collective-permute-start.13) | collective-permute-done | bytes 8224 | tf_op jit(solution)/shard_map/ppermute | solution.py:341
  37.2 1.6 %last.1 = (f32[1024,128]{1,0:T(8,128)}, f32[16,128]{1,0:T(8,128)}) custom-call(f32[1024,128]{1,0:T(8,128)S(1)} %get-tuple-element.45.done, bf16[128,128]{1,0:T(8,128)(2,1)S(1)} %get-tuple-element.46.matrix, f32[16,128]{1,0:T(8,128)S(1)} %get-tuple-element.47.kept, bf16[1040,128]{1,0:T(8,128)(2,1)S(1)} %collective-permute-done.12.far, ...), custom_call_target="tpu_custom_call" | custom-call | flops 67108864 | bytes 1310720 | tf_op jit(solution)/shard_map/last/pallas_call | solution.py:321
  (18 shorter events, 0.7 us)
Async XLA Ops:
  2.8 11.5 %collective-permute-start.10 = (bf16[256,128]{1,0:T(8,128)(2,1)S(1)}, bf16[256,128]{1,0:T(8,128)(2,1)S(1)}, u32[]{:S(2)}, u32[]{:S(2)}) collective-permute-start(bf16[256,128]{1,0:T(8,128)(2,1)S(1)} %get-tuple-element.53), channel_id=1, source_target_pairs={{0,6},{1,7},{2,4},{3,5},{4,2},{5,3},{6,0},{7,1},{8,14},{9,15},{10,... | collective-permute-start | bytes 196616 | tf_op jit(solution)/shard_map/ppermute | solution.py:356
  6.9 6.0 %collective-permute-start.7 = (s32[1,4224]{1,0:T(1,128)S(1)}, s32[1,4224]{1,0:T(1,128)S(1)}, u32[]{:S(2)}, u32[]{:S(2)}) collective-permute-start(s32[1,4224]{1,0:T(1,128)S(1)} %get-tuple-element.31.notes), channel_id=1, source_target_pairs={{0,8},{1,9},{2,10},{3,11},{4,12},{5,13},{6,14},{7,15},{8,0},{9,1},... | collective-permute-start | bytes 50696 | tf_op jit(solution)/shard_map/ppermute | solution.py:356
  9.5 13.3 %collective-permute-start = (bf16[512,128]{1,0:T(8,128)(2,1)S(1)}, bf16[512,128]{1,0:T(8,128)(2,1)S(1)}, u32[]{:S(2)}, u32[]{:S(2)}) collective-permute-start(bf16[512,128]{1,0:T(8,128)(2,1)S(1)} %get-tuple-element.36), channel_id=1, source_target_pairs={{0,1},{1,0},{2,3},{3,2},{4,5},{5,4},{6,7},{7,6},{8,9},{9,8},{10,11... | collective-permute-start | bytes 393224 | tf_op jit(solution)/shard_map/ppermute | solution.py:356
  11.0 6.4 %collective-permute-start.11 = (bf16[256,128]{1,0:T(8,128)(2,1)S(1)}, bf16[256,128]{1,0:T(8,128)(2,1)S(1)}, u32[]{:S(2)}, u32[]{:S(2)}) collective-permute-start(bf16[256,128]{1,0:T(8,128)(2,1)S(1)} %get-tuple-element.54), channel_id=1, source_target_pairs={{0,7},{1,6},{2,5},{3,4},{4,3},{5,2},{6,1},{7,0},{8,15},{9,14},{10,... | collective-permute-start | bytes 196616 | tf_op jit(solution)/shard_map/ppermute | solution.py:356
  11.3 11.4 %collective-permute-start.1 = (bf16[512,128]{1,0:T(8,128)(2,1)S(1)}, bf16[512,128]{1,0:T(8,128)(2,1)S(1)}, u32[]{:S(2)}, u32[]{:S(2)}) collective-permute-start(bf16[512,128]{1,0:T(8,128)(2,1)S(1)} %get-tuple-element.37), channel_id=1, source_target_pairs={{0,2},{1,3},{2,0},{3,1},{4,6},{5,7},{6,4},{7,5},{8,10},{9,11},{10,... | collective-permute-start | bytes 393224 | tf_op jit(solution)/shard_map/ppermute | solution.py:356
  12.8 9.9 %collective-permute-start.2 = (bf16[512,128]{1,0:T(8,128)(2,1)S(1)}, bf16[512,128]{1,0:T(8,128)(2,1)S(1)}, u32[]{:S(2)}, u32[]{:S(2)}) collective-permute-start(bf16[512,128]{1,0:T(8,128)(2,1)S(1)} %get-tuple-element.38), channel_id=1, source_target_pairs={{0,3},{1,2},{2,1},{3,0},{4,7},{5,6},{6,5},{7,4},{8,11},{9,10},{10,... | collective-permute-start | bytes 393224 | tf_op jit(solution)/shard_map/ppermute | solution.py:356
  14.3 5.0 %collective-permute-start.8 = (bf16[256,128]{1,0:T(8,128)(2,1)S(1)}, bf16[256,128]{1,0:T(8,128)(2,1)S(1)}, u32[]{:S(2)}, u32[]{:S(2)}) collective-permute-start(bf16[256,128]{1,0:T(8,128)(2,1)S(1)} %get-tuple-element.51), channel_id=1, source_target_pairs={{0,4},{1,5},{2,6},{3,7},{4,0},{5,1},{6,2},{7,3},{8,12},{9,13},{10,... | collective-permute-start | bytes 196616 | tf_op jit(solution)/shard_map/ppermute | solution.py:356
  17.4 5.4 %collective-permute-start.9 = (bf16[256,128]{1,0:T(8,128)(2,1)S(1)}, bf16[256,128]{1,0:T(8,128)(2,1)S(1)}, u32[]{:S(2)}, u32[]{:S(2)}) collective-permute-start(bf16[256,128]{1,0:T(8,128)(2,1)S(1)} %get-tuple-element.52), channel_id=1, source_target_pairs={{0,5},{1,4},{2,7},{3,6},{4,1},{5,0},{6,3},{7,2},{8,13},{9,12},{10,... | collective-permute-start | bytes 196616 | tf_op jit(solution)/shard_map/ppermute | solution.py:356
  19.2 8.1 %collective-permute-start.3 = (bf16[1024,128]{1,0:T(8,128)(2,1)S(1)}, bf16[1024,128]{1,0:T(8,128)(2,1)S(1)}, u32[]{:S(2)}, u32[]{:S(2)}) collective-permute-start(bf16[1024,128]{1,0:T(8,128)(2,1)S(1)} %get-tuple-element.39), channel_id=1, source_target_pairs={{0,4},{1,5},{2,6},{3,7},{4,0},{5,1},{6,2},{7,3},{8,12},{9,13},{10,... | collective-permute-start | bytes 786440 | tf_op jit(solution)/shard_map/ppermute | solution.py:356
  23.8 13.4 %collective-permute-start.12 = (bf16[1040,128]{1,0:T(8,128)(2,1)S(1)}, bf16[1040,128]{1,0:T(8,128)(2,1)S(1)}, u32[]{:S(2)}, u32[]{:S(2)}) collective-permute-start(bf16[1040,128]{1,0:T(8,128)(2,1)S(1)} %get-tuple-element.55), channel_id=1, source_target_pairs={{0,8},{1,9},{2,10},{3,11},{4,12},{5,13},{6,14},{7,15},{8,0},{9,1},... | collective-permute-start | bytes 798728 | tf_op jit(solution)/shard_map/ppermute | solution.py:356
  27.3 5.2 %collective-permute-start.4 = (bf16[256,128]{1,0:T(8,128)(2,1)S(1)}, bf16[256,128]{1,0:T(8,128)(2,1)S(1)}, u32[]{:S(2)}, u32[]{:S(2)}) collective-permute-start(bf16[256,128]{1,0:T(8,128)(2,1)S(1)} %get-tuple-element.42), channel_id=1, source_target_pairs={{0,1},{1,0},{2,3},{3,2},{4,5},{5,4},{6,7},{7,6},{8,9},{9,8},{10,11... | collective-permute-start | bytes 196616 | tf_op jit(solution)/shard_map/ppermute | solution.py:356
  27.6 4.8 %collective-permute-start.5 = (bf16[256,128]{1,0:T(8,128)(2,1)S(1)}, bf16[256,128]{1,0:T(8,128)(2,1)S(1)}, u32[]{:S(2)}, u32[]{:S(2)}) collective-permute-start(bf16[256,128]{1,0:T(8,128)(2,1)S(1)} %get-tuple-element.43), channel_id=1, source_target_pairs={{0,2},{1,3},{2,0},{3,1},{4,6},{5,7},{6,4},{7,5},{8,10},{9,11},{10,... | collective-permute-start | bytes 196616 | tf_op jit(solution)/shard_map/ppermute | solution.py:356
  29.4 5.2 %collective-permute-start.6 = (bf16[256,128]{1,0:T(8,128)(2,1)S(1)}, bf16[256,128]{1,0:T(8,128)(2,1)S(1)}, u32[]{:S(2)}, u32[]{:S(2)}) collective-permute-start(bf16[256,128]{1,0:T(8,128)(2,1)S(1)} %get-tuple-element.44), channel_id=1, source_target_pairs={{0,3},{1,2},{2,1},{3,0},{4,7},{5,6},{6,5},{7,4},{8,11},{9,10},{10,... | collective-permute-start | bytes 196616 | tf_op jit(solution)/shard_map/ppermute | solution.py:356
  31.8 2.8 %copy-start = (bf16[1,128,128]{2,1,0:T(8,128)(2,1)S(1)}, bf16[1,128,128]{2,1,0:T(8,128)(2,1)}, u32[]{:S(2)}) copy-start(bf16[1,128,128]{2,1,0:T(8,128)(2,1)} %param.7) | copy-start | bytes 98308
  31.8 2.7 %copy-start.1 = (s32[16]{0:T(128)S(1)}, s32[16]{0:T(128)}, u32[]{:S(2)}) copy-start(s32[16]{0:T(128)} %widths.1) | copy-start | bytes 196
  31.8 4.2 %collective-permute-start.14 = (f32[16,128]{1,0:T(8,128)S(1)}, f32[16,128]{1,0:T(8,128)S(1)}, u32[]{:S(2)}, u32[]{:S(2)}) collective-permute-start(f32[16,128]{1,0:T(8,128)S(1)} %get-tuple-element.57), channel_id=1, source_target_pairs={{0,24},{1,25},{2,26},{3,27},{4,28},{5,29},{6,30},{7,31},{8,16},{9,... | collective-permute-start | bytes 24584 | tf_op jit(solution)/shard_map/ppermute | solution.py:369
  35.9 1.2 %collective-permute-start.13 = (f32[16,128]{1,0:T(8,128)S(1)}, f32[16,128]{1,0:T(8,128)S(1)}, u32[]{:S(2)}, u32[]{:S(2)}) collective-permute-start(f32[16,128]{1,0:T(8,128)S(1)} %get-tuple-element.56), channel_id=1, source_target_pairs={{0,16},{16,0},{1,17},{17,1},{2,18},{18,2},{3,19},{19,3},{4,20},{20... | collective-permute-start | bytes 24584 | tf_op jit(solution)/shard_map/ppermute | solution.py:341

commit v2 on v1

--- a/solution.py
+++ b/solution.py
@@ -1,3 +1,4 @@
+import functools
 import math
 
 import jax
@@ -39,6 +40,7 @@
 
 def prep_body(grads, lookups, hot, notes, *refs):
     outs, (held, listed, sems, note_sems) = refs[:-4], refs[-4:]
+    planes = outs[SUB:-1]
     spd = grads.shape[0]
     me = lax.axis_index("tab")
     chunks = sems.shape[0]
@@ -65,6 +67,8 @@
                     rows = turned[at * STEP:(at + 1) * STEP]
                     if group == 0:
                         outs[at][pl.ds(low, STEP), :] = rows
+                    elif at in SPLIT:
+                        planes[SPLIT.index(at)][pl.ds(low, STEP), :] = rows
                     elif at < SUB // 2:
                         outs[at][pl.ds(spd + low, STEP), :] = rows
                     else:
@@ -85,11 +89,11 @@
     return pl.pallas_call(
         prep_body,
         out_shape=(jax.ShapeDtypeStruct((1, lookups.shape[1] + LANES), jnp.int32),)
-        + (block(2),) * half
-        + (block(1),) * half
+        + tuple(block(1 if shift in SPLIT or shift >= half else 2) for shift in range(SUB))
+        + (block(1),) * len(SPLIT)
         + (block(half),),
         in_specs=[HB] * 3,
-        out_specs=(VM,) * (SUB + 2),
+        out_specs=(VM,) * (SUB + 2 + len(SPLIT)),
         scratch_shapes=[
             pltpu.VMEM((spd, 2, SUB, width), jnp.bfloat16),
             pltpu.VMEM((1, hot.shape[1]), jnp.int32),
@@ -102,7 +106,7 @@
     )(*kept)
 
 
-def match_body(notes, low_match, high_side, hot_match):
+def fill_match(notes, low_match, high_side, hot_match):
     total = low_match.shape[1]
     size = LANES
     half = lax.axis_index("tab") // (lax.axis_size("tab") // 2)
@@ -128,7 +132,7 @@
 
 def match(notes, total, hots):
     return pl.pallas_call(
-        match_body,
+        fill_match,
         out_shape=(
             jax.ShapeDtypeStruct((LOW, total), jnp.bfloat16),
             jax.ShapeDtypeStruct((total, LANES), jnp.bfloat16),
@@ -141,19 +145,6 @@
     )(notes)
 
 
-def gather(spd, pieces, high_side, both, rows):
-    width = rows.shape[1]
-    near = lax.axis_size("tab") // 2
-    me = lax.axis_index("tab") % near
-    for shift, chunk, first in pieces:
-        where = pl.ds(pl.multiple_of((me ^ shift) * spd, spd), spd)
-        piece = chunk[pl.ds(first, spd), :]
-        upper = piece * high_side[where, :]
-        both[where, :width] = piece - upper
-        both[where, width:] = upper
-        rows[where, :] = piece
-
-
 def split(value):
     half = value.shape[0] // 2
     lower, upper = value[:half], value[half:]
@@ -161,42 +152,6 @@
     return jnp.where(first, lower, upper), jnp.where(first, upper, lower)
 
 
-def other_body(low_match, high_side, hot_match, *refs):
-    chunks, (out, given, both, rows) = refs[:-4], refs[-4:]
-    spd = rows.shape[0] // len(chunks)
-    gather(spd, [(at, chunk, 0) for at, chunk in enumerate(chunks)], high_side, both, rows)
-    width = rows.shape[1]
-    hot = jnp.dot(hot_match[...], rows[...], preferred_element_type=jnp.float32)
-    kept, given[...] = split(hot)
-    part = jnp.dot(low_match[...], both[...], preferred_element_type=jnp.float32)
-    for top in range(2):
-        out[pl.ds(top * LOW, LOW), :] = part[:, top * width:(top + 1) * width].astype(jnp.bfloat16)
-    out[pl.ds(ROWS, kept.shape[0]), :] = kept.astype(jnp.bfloat16)
-
-
-def scratch(matched, width):
-    total = matched[1].shape[0]
-    return [pltpu.VMEM((total, 2 * width), jnp.bfloat16), pltpu.VMEM((total, width), jnp.bfloat16)]
-
-
-def other_sums(chunks, matched):
-    width = chunks[0].shape[1]
-    total, half = matched[1].shape[0], matched[2].shape[0] // 2
-    return pl.pallas_call(
-        other_body,
-        out_shape=(
-            jax.ShapeDtypeStruct((ROWS + half, width), jnp.bfloat16),
-            jax.ShapeDtypeStruct((half, width), jnp.float32),
-        ),
-        in_specs=[VM] * (3 + len(chunks)),
-        out_specs=(VM, VM),
-        scratch_shapes=scratch(matched, width),
-        compiler_params=room(8),
-        cost_estimate=cost(2 * total * width * ROWS, total * width * 2),
-        name="other_sums",
-    )(*matched, *chunks)
-
-
 def project(values, matrix):
     high = values.astype(jnp.bfloat16)
     low = (values - high.astype(jnp.float32)).astype(jnp.bfloat16)
@@ -205,13 +160,15 @@
     )
 
 
-def partial_sums(spd, pieces, low_match, high_side, hot_match):
+def partial_sums(spd, pieces, low_match, high_side, hot_match, matrix=None):
     near = lax.axis_size("tab") // 2
     me = lax.axis_index("tab") % near
     sides, lows, hots, rows = [], [], [], []
-    for shift, chunk, first in pieces:
+    for shift, first, chunk in pieces:
         where = pl.ds(pl.multiple_of((me ^ shift) * spd, spd), spd)
         piece = chunk[pl.ds(first, spd), :]
+        if matrix is not None:
+            piece = jnp.dot(piece, matrix, preferred_element_type=jnp.float32).astype(jnp.bfloat16)
         upper = piece * high_side[where, :]
         sides.append(jnp.concatenate([piece - upper, upper], axis=1))
         lows.append(low_match[:, where])
@@ -222,61 +179,96 @@
     return both, hot
 
 
-def early_body(low_match, high_side, hot_match, own, one, two, three, relayed, total, hot):
-    spd = own.shape[0] // 2
-    pieces = [(0, own, spd), (1, one, spd), (2, two, spd), (3, three, spd), (4, relayed, 0)]
+def early_body(spd, places, low_match, high_side, hot_match, *refs):
+    chunks, (total, hot) = refs[:-2], refs[-2:]
+    pieces = [place + (chunk,) for place, chunk in zip(places, chunks)]
     total[...], hot[...] = partial_sums(spd, pieces, low_match, high_side, hot_match)
 
 
-def early_sums(matched, chunks):
-    width = chunks[0].shape[1]
-    count = matched[1].shape[0]
-    return pl.pallas_call(
-        early_body,
-        out_shape=(
-            jax.ShapeDtypeStruct((LOW, 2 * width), jnp.float32),
-            jax.ShapeDtypeStruct((matched[2].shape[0], width), jnp.float32),
-        ),
-        in_specs=[VM] * 8,
-        out_specs=(VM, VM),
-        compiler_params=room(8),
-        cost_estimate=cost(count * width * ROWS, count * width * 2),
-        name="early_sums",
-    )(*matched, *chunks)
-
-
-def own_body(widths, proj, low_match, high_side, hot_match, total, hot, *refs):
-    chunks, (done, matrix, kept, given) = refs[:-4], refs[-4:]
-    spd, width = chunks[0].shape
+def own_early_body(spd, places, widths, proj, low_match, high_side, hot_match, *refs):
+    chunks, (total, hot, matrix) = refs[:-3], refs[-3:]
     columns = lax.broadcasted_iota(jnp.int32, proj.shape, 1)
     limit = widths[lax.axis_index("tab")]
     matrix[...] = jnp.where(columns < limit, proj[...].astype(jnp.float32), 0.0).astype(jnp.bfloat16)
-    pieces = [(5 + at, chunk, 0) for at, chunk in enumerate(chunks)]
+    pieces = [place + (chunk,) for place, chunk in zip(places, chunks)]
+    total[...], hot[...] = partial_sums(spd, pieces, low_match, high_side, hot_match, matrix[...])
+
+
+def early_sums(spd, matched, items, widths=None, proj=None):
+    places, chunks = tuple(item[:2] for item in items), [item[2] for item in items]
+    width = chunks[0].shape[1]
+    shapes = (
+        jax.ShapeDtypeStruct((LOW, 2 * width), jnp.float32),
+        jax.ShapeDtypeStruct((matched[2].shape[0], width), jnp.float32),
+    )
+    own = proj is not None
+    if own:
+        shapes += (jax.ShapeDtypeStruct(proj.shape, jnp.bfloat16),)
+    return pl.pallas_call(
+        functools.partial(own_early_body if own else early_body, spd, places),
+        out_shape=shapes,
+        in_specs=([SM, VM] if own else []) + [VM] * (3 + len(chunks)),
+        out_specs=(VM,) * len(shapes),
+        compiler_params=room(8),
+        cost_estimate=cost(2 * spd * len(chunks) * width * ROWS, spd * len(chunks) * width * 2),
+        name="own_early" if own else "far_early",
+    )(*([widths, proj] if own else []), *matched, *chunks)
+
+
+def other_body(spd, places, low_match, high_side, hot_match, total, hot, *refs):
+    chunks, (lower, upper, given) = refs[:-3], refs[-3:]
+    pieces = [place + (chunk,) for place, chunk in zip(places, chunks)]
     both, more = partial_sums(spd, pieces, low_match, high_side, hot_match)
+    both += total[...]
+    width = lower.shape[1]
+    kept, given[...] = split(hot[...] + more)
+    lower[...] = both[:, :width].astype(jnp.bfloat16)
+    upper[pl.ds(0, LOW), :] = both[:, width:].astype(jnp.bfloat16)
+    upper[pl.ds(LOW, kept.shape[0]), :] = kept.astype(jnp.bfloat16)
+
+
+def other_sums(spd, matched, early, items):
+    places, chunks = tuple(item[:2] for item in items), [item[2] for item in items]
+    width, half = chunks[0].shape[1], matched[2].shape[0] // 2
+    return pl.pallas_call(
+        functools.partial(other_body, spd, places),
+        out_shape=(
+            jax.ShapeDtypeStruct((LOW, width), jnp.bfloat16),
+            jax.ShapeDtypeStruct((LOW + half, width), jnp.bfloat16),
+            jax.ShapeDtypeStruct((half, width), jnp.float32),
+        ),
+        in_specs=[VM] * (5 + len(chunks)),
+        out_specs=(VM,) * 3,
+        compiler_params=room(8),
+        cost_estimate=cost(2 * spd * len(chunks) * width * ROWS, spd * len(chunks) * width * 2),
+        name="other_sums",
+    )(*matched, *early, *chunks)
+
+
+def own_body(spd, places, matrix, low_match, high_side, hot_match, total, hot, *refs):
+    chunks, (done, kept, given) = refs[:-3], refs[-3:]
+    pieces = [place + (chunk,) for place, chunk in zip(places, chunks)]
+    both, more = partial_sums(spd, pieces, low_match, high_side, hot_match, matrix[...])
     kept[...], given[...] = split(hot[...] + more)
-    both += total[...]
+    width = done.shape[1]
     for top in range(2):
-        done[pl.ds(top * LOW, LOW), :] = project(both[:, top * width:(top + 1) * width], matrix[...])
-
-
-def own_sums(matched, early, chunks, proj, widths):
-    width = chunks[0].shape[1]
-    count, half = matched[1].shape[0], matched[2].shape[0] // 2
+        where = slice(top * width, (top + 1) * width)
+        done[pl.ds(top * LOW, LOW), :] = both[:, where] + total[:, where]
+
+
+def own_sums(spd, matched, early, items, matrix):
+    places, chunks = tuple(item[:2] for item in items), [item[2] for item in items]
+    width, half = chunks[0].shape[1], matched[2].shape[0] // 2
     part = jax.ShapeDtypeStruct((half, width), jnp.float32)
     return pl.pallas_call(
-        own_body,
-        out_shape=(
-            jax.ShapeDtypeStruct((ROWS, width), jnp.float32),
-            jax.ShapeDtypeStruct((width, width), jnp.bfloat16),
-            part,
-            part,
-        ),
-        in_specs=[SM] + [VM] * (6 + len(chunks)),
-        out_specs=(VM,) * 4,
+        functools.partial(own_body, spd, places),
+        out_shape=(jax.ShapeDtypeStruct((ROWS, width), jnp.float32), part, part),
+        in_specs=[VM] * (6 + len(chunks)),
+        out_specs=(VM,) * 3,
         compiler_params=room(8),
-        cost_estimate=cost(count * width * ROWS, count * width * 2),
+        cost_estimate=cost(2 * spd * len(chunks) * width * ROWS, spd * len(chunks) * width * 2),
         name="own_sums",
-    )(widths, proj, *matched, *early, *chunks)
+    )(matrix, *matched, *early, *chunks)
 
 
 def cut_body(block, *outs):
@@ -298,42 +290,71 @@
     )(block)
 
 
-PIECES = 4
-
-
-def last_body(done, matrix, kept, far, same_chip, far_chip, cold, hot, held, sems):
-    size = ROWS // PIECES
-    table = matrix[...]
+PIECES = 2
+
+
+def write_rows(top, done, table, far, cold, held, sems):
+    size = LOW // PIECES
     moves = []
     for piece in range(PIECES):
-        where = pl.ds(piece * size, size)
-        held[where, :] = done[where, :] + jnp.dot(far[where, :], table, preferred_element_type=jnp.float32)
-        moves.append(pltpu.make_async_copy(held.at[where], cold.at[where], sems.at[piece]))
+        where = pl.ds(top * LOW + piece * size, size)
+        from_far = pl.ds(piece * size, size)
+        held[from_far, :] = done[where, :] + jnp.dot(far[from_far, :], table, preferred_element_type=jnp.float32)
+        moves.append(pltpu.make_async_copy(held.at[from_far], cold.at[where], sems.at[piece]))
         moves[-1].start()
-    hot_far = far[pl.ds(ROWS, hot.shape[0]), :].astype(jnp.float32)
-    hot[...] = project(kept[...] + hot_far + same_chip[...] + far_chip[...], table)
+    return moves
+
+
+def lower_body(done, matrix, far, cold, held, sems):
+    for one in write_rows(0, done, matrix[...], far, cold, held, sems):
+        one.wait()
+
+
+def last_scratch(width):
+    return [pltpu.VMEM((LOW, width), jnp.float32), pltpu.SemaphoreType.DMA((PIECES,))]
+
+
+def lower_part(done, matrix, far):
+    width = far.shape[1]
+    return pl.pallas_call(
+        lower_body,
+        out_shape=jax.ShapeDtypeStruct((ROWS, width), jnp.float32),
+        in_specs=[VM] * 3,
+        out_specs=HB,
+        scratch_shapes=last_scratch(width),
+        compiler_params=room(4),
+        cost_estimate=cost(2 * ROWS * width * width, ROWS * width * 5),
+        name="lower_part",
+    )(done, matrix, far)
+
+
+def upper_body(begun, done, matrix, kept, far, same_chip, far_chip, cold, hot, held, sems, hot_held, hot_sem):
+    table = matrix[...]
+    hot_far = far[pl.ds(LOW, hot.shape[0]), :].astype(jnp.float32)
+    hot_held[...] = kept[...] + same_chip[...] + project(hot_far + far_chip[...], table)
+    moves = [pltpu.make_async_copy(hot_held, hot, hot_sem)]
+    moves[0].start()
+    moves += write_rows(1, done, table, far, cold, held, sems)
     for one in moves:
         one.wait()
 
 
-def last(done, matrix, kept, far, same_chip, far_chip):
+def upper_part(begun, done, matrix, kept, far, same_chip, far_chip):
     half, width = same_chip.shape
     return pl.pallas_call(
-        last_body,
+        upper_body,
         out_shape=(
             jax.ShapeDtypeStruct((ROWS, width), jnp.float32),
             jax.ShapeDtypeStruct((half, width), jnp.float32),
         ),
-        in_specs=[VM] * 6,
-        out_specs=(HB, VM),
-        scratch_shapes=[
-            pltpu.VMEM((ROWS, width), jnp.float32),
-            pltpu.SemaphoreType.DMA((PIECES,)),
-        ],
+        in_specs=[HB] + [VM] * 6,
+        out_specs=(HB, HB),
+        scratch_shapes=last_scratch(width) + [pltpu.VMEM((half, width), jnp.float32), pltpu.SemaphoreType.DMA],
+        input_output_aliases={0: 0},
         compiler_params=room(4),
-        cost_estimate=cost(4 * ROWS * width * width, ROWS * width * 10),
-        name="last",
-    )(done, matrix, kept, far, same_chip, far_chip)
+        cost_estimate=cost(2 * ROWS * width * width, ROWS * width * 5),
+        name="upper_part",
+    )(begun, done, matrix, kept, far, same_chip, far_chip)
 
 
 def swap_reps(block):
@@ -343,6 +364,8 @@
 
 FIRST = (7, 6, 5, 4, 3, 2, 1)
 PLANE = (1, 2, 3)
+SPLIT = ()
+EARLY = (0, 4, 3, 7, 6, 5)
 
 
 def shards(grad_out, indices, projections, widths, hot_ids):
@@ -362,8 +385,15 @@
     far_notes = send(notes, SUB)
     relayed = send(relay, SUB // 2)
     far_matched = match(far_notes, half_len, hots)
-    partial, far_given = other_sums([got[shift] for shift in range(SUB)], far_matched)
-    far = send(partial, SUB)
+    far_early = early_sums(spd, far_matched, [(shift, 0, got[shift]) for shift in EARLY])
+    lower, upper, far_given = other_sums(
+        spd, far_matched, far_early, [(shift, 0, got[shift]) for shift in range(SUB) if shift not in EARLY]
+    )
+    far_lower = send(lower, SUB)
+    far_upper = send(upper, SUB)
+    own = [(shift, spd, got[shift]) for shift in (0,) + PLANE if shift not in SPLIT]
+    own += [(shift, 0, send(block, shift)) for shift, block in zip(SPLIT, blocks[SUB:])]
+    own += [(SUB // 2, 0, relayed)]
     pieces = cut(relayed, SUB // 2)
     second = [send(pieces[shift - 1], shift) for shift in PLANE]
     far_chip = lax.ppermute(
@@ -372,10 +402,13 @@
         [(r * count + i, (r ^ 1) * count + (i ^ SUB)) for r in range(reps) for i in range(count)],
     )
     own_matched = match(notes, half_len, hots)
-    early = early_sums(own_matched, [got[0], got[1], got[2], got[3], relayed])
-    done, matrix, kept, given = own_sums(own_matched, early, second, projections[0], widths)
+    *own_early, matrix = early_sums(spd, own_matched, own, widths, projections[0])
+    done, kept, given = own_sums(
+        spd, own_matched, own_early, [(SUB // 2 + shift, 0, one) for shift, one in zip(PLANE, second)], matrix
+    )
     same_chip = swap_reps(given)
-    cold, hot = last(done, matrix, kept, far, same_chip, far_chip)
+    begun = lower_part(done, matrix, far_lower)
+    cold, hot = upper_part(begun, done, matrix, kept, far_upper, same_chip, far_chip)
     return cold[None, None], hot[None]
 
 

time: 38.9 us -> 41.5 us (1.067)
  the two profiles are of different devices: /device:TPU:0 before, /device:TPU:9 now
where the time goes in v2:
time: 41.5 us; the launch traced here: 41 us
  starting transfers between devices  23.3 us (56%)
  Pallas kernels  8.69 us (21%)
  waiting for transfers between devices  8.26 us (20%)
  between operations  0.8 us (2%)
    ppermute x14, starting transfers between devices, send(): return lax.ppermute(block, 'tab', [(i, i ^ shift) for i in range(count)])  15.2 us
    ppermute x14, waiting for transfers between devices, send(): return lax.ppermute(block, 'tab', [(i, i ^ shift) for i in range(count)])  8.25 us
    ppermute x1, starting transfers between devices, shards(): lax.ppermute(far_given, ('rep', 'tab'), [(r * count + i, (r ^ 1) * count...  5.69 us
    ppermute x1, starting transfers between devices, swap_reps(): return lax.ppermute(block, 'rep', [(r, r ^ 1) for r in range(reps)])  2.34 us
    pallas_call x1, Pallas kernels, prep(): pl.pallas_call(prep_body, out_shape=(jax.ShapeDtypeStruct((1, lookups.sha...  2.16 us
    pallas_call x2, Pallas kernels, early_sums(): pl.pallas_call(functools.partial(own_early_body if own else early_body, s...  1.97 us
    pallas_call x2, Pallas kernels, match(): pl.pallas_call(fill_match, out_shape=(jax.ShapeDtypeStruct((LOW, total),...  1.83 us
    pallas_call x1, Pallas kernels, upper_part(): pl.pallas_call(upper_body, out_shape=(jax.ShapeDtypeStruct((ROWS, width),...  0.92 us
  transfers between devices with their start and end apart: 16, of which 2 were waited for; matrix products, arithmetic and copies ran while one was open for 0% of the time, Pallas kernels for 14%

profile of v2, /device:TPU:9, one launch (start us, length us, event | category | flops | bytes accessed | tf_op | source)
XLA Modules:
  0.0 41.0 jit_solution(8530714575330055614)
XLA Ops:
  0.6 2.2 %prep.1 = (s32[1,4224]{1,0:T(1,128)S(1)}, bf16[512,128]{1,0:T(8,128)(2,1)S(1)}, bf16[512,128]{1,0:T(8,128)(2,1)S(1)}, bf16[512,128]{1,0:T(8,128)(2,1)S(1)}, bf16...) custom-call(bf16[256,2,8,128]{3,2,1,0:T(8,128)(2,1)} %bitcast.6, ...), custom_call_target="tpu_custom_call" | custom-call | flops 268435456 | bytes 2097152 | tf_op jit(solution)/shard_map/prep/pallas_call | solution.py:89
  2.9 2.4 %collective-permute-start.10 = (bf16[256,128]{1,0:T(8,128)(2,1)S(1)}, bf16[256,128]{1,0:T(8,128)(2,1)S(1)}, u32[]{:S(2)}, u32[]{:S(2)}) collective-permute-start(bf16[256,128]{1,0:T(8,128)(2,1)S(1)} %get-tuple-element.55), channel_id=1, source_target_pairs={{0,6},{1,7},{2,4},{3,5},{4,2},{5,3},{6,0},{7,1},{8,14},{9,15},{10,... | collective-permute-start | bytes 196616 | tf_op jit(solution)/shard_map/ppermute | solution.py:379
  5.3 1.1 %collective-permute-start.11 = (bf16[256,128]{1,0:T(8,128)(2,1)S(1)}, bf16[256,128]{1,0:T(8,128)(2,1)S(1)}, u32[]{:S(2)}, u32[]{:S(2)}) collective-permute-start(bf16[256,128]{1,0:T(8,128)(2,1)S(1)} %get-tuple-element.56), channel_id=1, source_target_pairs={{0,5},{1,4},{2,7},{3,6},{4,1},{5,0},{6,3},{7,2},{8,13},{9,12},{10,... | collective-permute-start | bytes 196616 | tf_op jit(solution)/shard_map/ppermute | solution.py:379
  6.4 2.3 %collective-permute-start.7 = (s32[1,4224]{1,0:T(1,128)S(1)}, s32[1,4224]{1,0:T(1,128)S(1)}, u32[]{:S(2)}, u32[]{:S(2)}) collective-permute-start(s32[1,4224]{1,0:T(1,128)S(1)} %get-tuple-element.34.notes), channel_id=1, source_target_pairs={{0,8},{1,9},{2,10},{3,11},{4,12},{5,13},{6,14},{7,15},{8,0},{9,1},... | collective-permute-start | bytes 50696 | tf_op jit(solution)/shard_map/ppermute | solution.py:379
  8.7 1.3 %collective-permute-start.8 = (bf16[256,128]{1,0:T(8,128)(2,1)S(1)}, bf16[256,128]{1,0:T(8,128)(2,1)S(1)}, u32[]{:S(2)}, u32[]{:S(2)}) collective-permute-start(bf16[256,128]{1,0:T(8,128)(2,1)S(1)} %get-tuple-element.53), channel_id=1, source_target_pairs={{0,4},{1,5},{2,6},{3,7},{4,0},{5,1},{6,2},{7,3},{8,12},{9,13},{10,... | collective-permute-start | bytes 196616 | tf_op jit(solution)/shard_map/ppermute | solution.py:379
  10.0 4.2 %collective-permute-done.7.notes = s32[1,4224]{1,0:T(1,128)S(1)} collective-permute-done((s32[1,4224]{1,0:T(1,128)S(1)}, s32[1,4224]{1,0:T(1,128)S(1)}, u32[]{:S(2)}, u32[]{:S(2)}) %collective-permute-start.7) | collective-permute-done | bytes 16928 | tf_op jit(solution)/shard_map/ppermute | solution.py:379
  14.2 2.2 %collective-permute-start.2 = (bf16[512,128]{1,0:T(8,128)(2,1)S(1)}, bf16[512,128]{1,0:T(8,128)(2,1)S(1)}, u32[]{:S(2)}, u32[]{:S(2)}) collective-permute-start(bf16[512,128]{1,0:T(8,128)(2,1)S(1)} %get-tuple-element.41), channel_id=1, source_target_pairs={{0,3},{1,2},{2,1},{3,0},{4,7},{5,6},{6,5},{7,4},{8,11},{9,10},{10,... | collective-permute-start | bytes 393224 | tf_op jit(solution)/shard_map/ppermute | solution.py:379
  16.4 0.5 %collective-permute-start.1 = (bf16[512,128]{1,0:T(8,128)(2,1)S(1)}, bf16[512,128]{1,0:T(8,128)(2,1)S(1)}, u32[]{:S(2)}, u32[]{:S(2)}) collective-permute-start(bf16[512,128]{1,0:T(8,128)(2,1)S(1)} %get-tuple-element.40), channel_id=1, source_target_pairs={{0,2},{1,3},{2,0},{3,1},{4,6},{5,7},{6,4},{7,5},{8,10},{9,11},{10,... | collective-permute-start | bytes 393224 | tf_op jit(solution)/shard_map/ppermute | solution.py:379
  17.0 0.9 %shard_map.69 = (bf16[512,2048]{1,0:T(8,128)(2,1)S(1)}, bf16[2048,128]{1,0:T(8,128)(2,1)S(1)}, bf16[32,2048]{1,0:T(8,128)(2,1)S(1)}) custom-call(s32[1,4224]{1,0:T(1,128)S(1)} %collective-permute-done.7.notes), custom_call_target="tpu_custom_call" | custom-call | flops 419430400 | bytes 2097152 | tf_op jit(solution)/shard_map/pallas_call | solution.py:134
  18.0 4.0 %collective-permute-done.9.refs_3_ = bf16[256,128]{1,0:T(8,128)(2,1)S(1)} collective-permute-done((bf16[256,128]{1,0:T(8,128)(2,1)S(1)}, bf16[256,128]{1,0:T(8,128)(2,1)S(1)}, u32[]{:S(2)}, u32[]{:S(2)}) %collective-permute-start.9) | collective-permute-done | bytes 65568 | tf_op jit(solution)/shard_map/ppermute | solution.py:379
  21.9 0.6 %far_early.1 = (f32[512,256]{1,0:T(8,128)S(1)}, f32[32,128]{1,0:T(8,128)S(1)}) custom-call(bf16[512,2048]{1,0:T(8,128)(2,1)S(1)} %get-tuple-element.50.low_match, bf16[2048,128]{1,0:T(8,128)(2,1)S(1)} %get-tuple-element.51.high_side, bf16[32,2048]{1,0:T(8,128)(2,1)S(1)} %get-tuple-element.52.hot_match, bf16[512,128]{1,0:T(8,128)(2,1)S(1)} %get-tuple-element.38.refs_0_, ...), custom_call_target="tpu_custom_call" | custom-call | flops 402653184 | bytes 393216 | tf_op jit(solution)/shard_map/far_early/pallas_call | solution.py:207
  22.6 0.3 other_sums.1
  23.0 0.7 %collective-permute-start.13 = (bf16[528,128]{1,0:T(8,128)(2,1)S(1)}, bf16[528,128]{1,0:T(8,128)(2,1)S(1)}, u32[]{:S(2)}, u32[]{:S(2)}) collective-permute-start(bf16[528,128]{1,0:T(8,128)(2,1)S(1)} %get-tuple-element.61), channel_id=1, source_target_pairs={{0,8},{1,9},{2,10},{3,11},{4,12},{5,13},{6,14},{7,15},{8,0},{9,1},... | collective-permute-start | bytes 405512 | tf_op jit(solution)/shard_map/ppermute | solution.py:379
  23.7 1.7 %collective-permute-start.12 = (bf16[512,128]{1,0:T(8,128)(2,1)S(1)}, bf16[512,128]{1,0:T(8,128)(2,1)S(1)}, u32[]{:S(2)}, u32[]{:S(2)}) collective-permute-start(bf16[512,128]{1,0:T(8,128)(2,1)S(1)} %get-tuple-element.59), channel_id=1, source_target_pairs={{0,8},{1,9},{2,10},{3,11},{4,12},{5,13},{6,14},{7,15},{8,0},{9,1},... | collective-permute-start | bytes 393224 | tf_op jit(solution)/shard_map/ppermute | solution.py:379
  25.4 1.6 %collective-permute-start.4 = (bf16[256,128]{1,0:T(8,128)(2,1)S(1)}, bf16[256,128]{1,0:T(8,128)(2,1)S(1)}, u32[]{:S(2)}, u32[]{:S(2)}) collective-permute-start(bf16[256,128]{1,0:T(8,128)(2,1)S(1)} %get-tuple-element.46), channel_id=1, source_target_pairs={{0,1},{1,0},{2,3},{3,2},{4,5},{5,4},{6,7},{7,6},{8,9},{9,8},{10,11... | collective-permute-start | bytes 196616 | tf_op jit(solution)/shard_map/ppermute | solution.py:379
  27.0 1.0 %collective-permute-start.5 = (bf16[256,128]{1,0:T(8,128)(2,1)S(1)}, bf16[256,128]{1,0:T(8,128)(2,1)S(1)}, u32[]{:S(2)}, u32[]{:S(2)}) collective-permute-start(bf16[256,128]{1,0:T(8,128)(2,1)S(1)} %get-tuple-element.47), channel_id=1, source_target_pairs={{0,2},{1,3},{2,0},{3,1},{4,6},{5,7},{6,4},{7,5},{8,10},{9,11},{10,... | collective-permute-start | bytes 196616 | tf_op jit(solution)/shard_map/ppermute | solution.py:379
  28.0 0.3 collective-permute-start.6
  28.3 0.9 %shard_map.68 = (bf16[512,2048]{1,0:T(8,128)(2,1)S(1)}, bf16[2048,128]{1,0:T(8,128)(2,1)S(1)}, bf16[32,2048]{1,0:T(8,128)(2,1)S(1)}) custom-call(s32[1,4224]{1,0:T(1,128)S(1)} %get-tuple-element.34.notes), custom_call_target="tpu_custom_call" | custom-call | flops 419430400 | bytes 2097152 | tf_op jit(solution)/shard_map/pallas_call | solution.py:134
  29.2 1.3 %own_early.1 = (f32[512,256]{1,0:T(8,128)S(1)}, f32[32,128]{1,0:T(8,128)S(1)}, bf16[128,128]{1,0:T(8,128)(2,1)S(1)}) custom-call(s32[16]{0:T(128)S(1)} %copy-done.1, bf16[128,128]{1,0:T(8,128)(2,1)S(1)} %bitcast.4, bf16[512,2048]{1,0:T(8,128)(2,1)S(1)} %get-tuple-element.35.low_match, bf16[2048,128]{1,0:T(8,128)(2,1)S(1)} %get-tuple-element.36.high_side, ...), custom_call_target="tpu_custom_call" | custom-call | flops 335544320 | bytes 327680 | tf_op jit(solution)/shard_map/own_early/pallas_call | solution.py:207
  30.5 5.7 %collective-permute-start.15 = (f32[16,128]{1,0:T(8,128)S(1)}, f32[16,128]{1,0:T(8,128)S(1)}, u32[]{:S(2)}, u32[]{:S(2)}) collective-permute-start(f32[16,128]{1,0:T(8,128)S(1)} %get-tuple-element.63), channel_id=1, source_target_pairs={{0,24},{1,25},{2,26},{3,27},{4,28},{5,29},{6,30},{7,31},{8,16},{9,... | collective-permute-start | bytes 24584 | tf_op jit(solution)/shard_map/ppermute | solution.py:399
  36.2 0.6 %own_sums.1 = (f32[1024,128]{1,0:T(8,128)S(1)}, f32[16,128]{1,0:T(8,128)S(1)}, f32[16,128]{1,0:T(8,128)S(1)}) custom-call(bf16[128,128]{1,0:T(8,128)(2,1)S(1)} %get-tuple-element.43.matrix, bf16[512,2048]{1,0:T(8,128)(2,1)S(1)} %get-tuple-element.35.low_match, bf16[2048,128]{1,0:T(8,128)(2,1)S(1)} %get-tuple-element.36.high_side, ...), custom_call_target="tpu_custom_call" | custom-call | flops 201326592 | bytes 196608 | tf_op jit(solution)/shard_map/own_sums/pallas_call | solution.py:263
  36.8 2.3 %collective-permute-start.14 = (f32[16,128]{1,0:T(8,128)S(1)}, f32[16,128]{1,0:T(8,128)S(1)}, u32[]{:S(2)}, u32[]{:S(2)}) collective-permute-start(f32[16,128]{1,0:T(8,128)S(1)} %get-tuple-element.62), channel_id=1, source_target_pairs={{0,16},{16,0},{1,17},{17,1},{2,18},{18,2},{3,19},{19,3},{4,20},{20... | collective-permute-start | bytes 24584 | tf_op jit(solution)/shard_map/ppermute | solution.py:362
  39.2 0.9 %lower_part.1.begun = f32[1024,128]{1,0:T(8,128)} custom-call(f32[1024,128]{1,0:T(8,128)S(1)} %get-tuple-element.49.done, bf16[128,128]{1,0:T(8,128)(2,1)S(1)} %get-tuple-element.43.matrix, bf16[512,128]{1,0:T(8,128)(2,1)S(1)} %collective-permute-done.12.far), custom_call_target="tpu_custom_call" | custom-call | flops 33554432 | bytes 655360 | tf_op jit(solution)/shard_map/lower_part/pallas_call | solution.py:319
  40.1 0.9 %upper_part.1 = (f32[1024,128]{1,0:T(8,128)}, f32[16,128]{1,0:T(8,128)}) custom-call(f32[1024,128]{1,0:T(8,128)} %lower_part.1.begun, f32[1024,128]{1,0:T(8,128)S(1)} %get-tuple-element.49.done, bf16[128,128]{1,0:T(8,128)(2,1)S(1)} %get-tuple-element.43.matrix, f32[16,128]{1,0:T(8,128)S(1)} %get-tuple-element.60.kept, ...), custom_call_target="tpu_custom_call", output_to_operand_aliasing={{0}: (0, {})} | custom-call | flops 33554432 | bytes 655360 | tf_op jit(solution)/shard_map/upper_part/pallas_call | solution.py:344
  (22 shorter events, 0.3 us)
Async XLA Ops:
  2.8 22.6 %collective-permute-start.3 = (bf16[1024,128]{1,0:T(8,128)(2,1)S(1)}, bf16[1024,128]{1,0:T(8,128)(2,1)S(1)}, u32[]{:S(2)}, u32[]{:S(2)}) collective-permute-start(bf16[1024,128]{1,0:T(8,128)(2,1)S(1)} %get-tuple-element.42), channel_id=1, source_target_pairs={{0,4},{1,5},{2,6},{3,7},{4,0},{5,1},{6,2},{7,3},{8,12},{9,13},{10,... | collective-permute-start | bytes 786440 | tf_op jit(solution)/shard_map/ppermute | solution.py:379
  2.9 13.5 %collective-permute-start.10 = (bf16[256,128]{1,0:T(8,128)(2,1)S(1)}, bf16[256,128]{1,0:T(8,128)(2,1)S(1)}, u32[]{:S(2)}, u32[]{:S(2)}) collective-permute-start(bf16[256,128]{1,0:T(8,128)(2,1)S(1)} %get-tuple-element.55), channel_id=1, source_target_pairs={{0,6},{1,7},{2,4},{3,5},{4,2},{5,3},{6,0},{7,1},{8,14},{9,15},{10,... | collective-permute-start | bytes 196616 | tf_op jit(solution)/shard_map/ppermute | solution.py:379
  5.3 11.1 %collective-permute-start.11 = (bf16[256,128]{1,0:T(8,128)(2,1)S(1)}, bf16[256,128]{1,0:T(8,128)(2,1)S(1)}, u32[]{:S(2)}, u32[]{:S(2)}) collective-permute-start(bf16[256,128]{1,0:T(8,128)(2,1)S(1)} %get-tuple-element.56), channel_id=1, source_target_pairs={{0,5},{1,4},{2,7},{3,6},{4,1},{5,0},{6,3},{7,2},{8,13},{9,12},{10,... | collective-permute-start | bytes 196616 | tf_op jit(solution)/shard_map/ppermute | solution.py:379
  6.4 7.9 %collective-permute-start.7 = (s32[1,4224]{1,0:T(1,128)S(1)}, s32[1,4224]{1,0:T(1,128)S(1)}, u32[]{:S(2)}, u32[]{:S(2)}) collective-permute-start(s32[1,4224]{1,0:T(1,128)S(1)} %get-tuple-element.34.notes), channel_id=1, source_target_pairs={{0,8},{1,9},{2,10},{3,11},{4,12},{5,13},{6,14},{7,15},{8,0},{9,1},... | collective-permute-start | bytes 50696 | tf_op jit(solution)/shard_map/ppermute | solution.py:379
  8.7 8.2 %collective-permute-start.8 = (bf16[256,128]{1,0:T(8,128)(2,1)S(1)}, bf16[256,128]{1,0:T(8,128)(2,1)S(1)}, u32[]{:S(2)}, u32[]{:S(2)}) collective-permute-start(bf16[256,128]{1,0:T(8,128)(2,1)S(1)} %get-tuple-element.53), channel_id=1, source_target_pairs={{0,4},{1,5},{2,6},{3,7},{4,0},{5,1},{6,2},{7,3},{8,12},{9,13},{10,... | collective-permute-start | bytes 196616 | tf_op jit(solution)/shard_map/ppermute | solution.py:379
  14.2 7.7 %collective-permute-start.2 = (bf16[512,128]{1,0:T(8,128)(2,1)S(1)}, bf16[512,128]{1,0:T(8,128)(2,1)S(1)}, u32[]{:S(2)}, u32[]{:S(2)}) collective-permute-start(bf16[512,128]{1,0:T(8,128)(2,1)S(1)} %get-tuple-element.41), channel_id=1, source_target_pairs={{0,3},{1,2},{2,1},{3,0},{4,7},{5,6},{6,5},{7,4},{8,11},{9,10},{10,... | collective-permute-start | bytes 393224 | tf_op jit(solution)/shard_map/ppermute | solution.py:379
  16.4 6.2 %collective-permute-start = (bf16[512,128]{1,0:T(8,128)(2,1)S(1)}, bf16[512,128]{1,0:T(8,128)(2,1)S(1)}, u32[]{:S(2)}, u32[]{:S(2)}) collective-permute-start(bf16[512,128]{1,0:T(8,128)(2,1)S(1)} %get-tuple-element.39), channel_id=1, source_target_pairs={{0,1},{1,0},{2,3},{3,2},{4,5},{5,4},{6,7},{7,6},{8,9},{9,8},{10,11... | collective-permute-start | bytes 393224 | tf_op jit(solution)/shard_map/ppermute | solution.py:379
  16.4 6.2 %collective-permute-start.1 = (bf16[512,128]{1,0:T(8,128)(2,1)S(1)}, bf16[512,128]{1,0:T(8,128)(2,1)S(1)}, u32[]{:S(2)}, u32[]{:S(2)}) collective-permute-start(bf16[512,128]{1,0:T(8,128)(2,1)S(1)} %get-tuple-element.40), channel_id=1, source_target_pairs={{0,2},{1,3},{2,0},{3,1},{4,6},{5,7},{6,4},{7,5},{8,10},{9,11},{10,... | collective-permute-start | bytes 393224 | tf_op jit(solution)/shard_map/ppermute | solution.py:379
  16.9 5.0 %collective-permute-start.9 = (bf16[256,128]{1,0:T(8,128)(2,1)S(1)}, bf16[256,128]{1,0:T(8,128)(2,1)S(1)}, u32[]{:S(2)}, u32[]{:S(2)}) collective-permute-start(bf16[256,128]{1,0:T(8,128)(2,1)S(1)} %get-tuple-element.54), channel_id=1, source_target_pairs={{0,7},{1,6},{2,5},{3,4},{4,3},{5,2},{6,1},{7,0},{8,15},{9,14},{10,... | collective-permute-start | bytes 196616 | tf_op jit(solution)/shard_map/ppermute | solution.py:379
  22.6 6.6 %copy-start = (bf16[1,128,128]{2,1,0:T(8,128)(2,1)S(1)}, bf16[1,128,128]{2,1,0:T(8,128)(2,1)}, u32[]{:S(2)}) copy-start(bf16[1,128,128]{2,1,0:T(8,128)(2,1)} %param.7) | copy-start | bytes 98308
  22.6 6.6 %copy-start.1 = (s32[16]{0:T(128)S(1)}, s32[16]{0:T(128)}, u32[]{:S(2)}) copy-start(s32[16]{0:T(128)} %widths.1) | copy-start | bytes 196
  23.0 17.1 %collective-permute-start.13 = (bf16[528,128]{1,0:T(8,128)(2,1)S(1)}, bf16[528,128]{1,0:T(8,128)(2,1)S(1)}, u32[]{:S(2)}, u32[]{:S(2)}) collective-permute-start(bf16[528,128]{1,0:T(8,128)(2,1)S(1)} %get-tuple-element.61), channel_id=1, source_target_pairs={{0,8},{1,9},{2,10},{3,11},{4,12},{5,13},{6,14},{7,15},{8,0},{9,1},... | collective-permute-start | bytes 405512 | tf_op jit(solution)/shard_map/ppermute | solution.py:379
  23.7 15.4 %collective-permute-start.12 = (bf16[512,128]{1,0:T(8,128)(2,1)S(1)}, bf16[512,128]{1,0:T(8,128)(2,1)S(1)}, u32[]{:S(2)}, u32[]{:S(2)}) collective-permute-start(bf16[512,128]{1,0:T(8,128)(2,1)S(1)} %get-tuple-element.59), channel_id=1, source_target_pairs={{0,8},{1,9},{2,10},{3,11},{4,12},{5,13},{6,14},{7,15},{8,0},{9,1},... | collective-permute-start | bytes 393224 | tf_op jit(solution)/shard_map/ppermute | solution.py:379
  25.4 5.1 %collective-permute-start.4 = (bf16[256,128]{1,0:T(8,128)(2,1)S(1)}, bf16[256,128]{1,0:T(8,128)(2,1)S(1)}, u32[]{:S(2)}, u32[]{:S(2)}) collective-permute-start(bf16[256,128]{1,0:T(8,128)(2,1)S(1)} %get-tuple-element.46), channel_id=1, source_target_pairs={{0,1},{1,0},{2,3},{3,2},{4,5},{5,4},{6,7},{7,6},{8,9},{9,8},{10,11... | collective-permute-start | bytes 196616 | tf_op jit(solution)/shard_map/ppermute | solution.py:379
  27.0 9.2 %collective-permute-start.5 = (bf16[256,128]{1,0:T(8,128)(2,1)S(1)}, bf16[256,128]{1,0:T(8,128)(2,1)S(1)}, u32[]{:S(2)}, u32[]{:S(2)}) collective-permute-start(bf16[256,128]{1,0:T(8,128)(2,1)S(1)} %get-tuple-element.47), channel_id=1, source_target_pairs={{0,2},{1,3},{2,0},{3,1},{4,6},{5,7},{6,4},{7,5},{8,10},{9,11},{10,... | collective-permute-start | bytes 196616 | tf_op jit(solution)/shard_map/ppermute | solution.py:379
  28.0 8.2 %collective-permute-start.6 = (bf16[256,128]{1,0:T(8,128)(2,1)S(1)}, bf16[256,128]{1,0:T(8,128)(2,1)S(1)}, u32[]{:S(2)}, u32[]{:S(2)}) collective-permute-start(bf16[256,128]{1,0:T(8,128)(2,1)S(1)} %get-tuple-element.48), channel_id=1, source_target_pairs={{0,3},{1,2},{2,1},{3,0},{4,7},{5,6},{6,5},{7,4},{8,11},{9,10},{10,... | collective-permute-start | bytes 196616 | tf_op jit(solution)/shard_map/ppermute | solution.py:379
  30.5 9.5 %collective-permute-start.15 = (f32[16,128]{1,0:T(8,128)S(1)}, f32[16,128]{1,0:T(8,128)S(1)}, u32[]{:S(2)}, u32[]{:S(2)}) collective-permute-start(f32[16,128]{1,0:T(8,128)S(1)} %get-tuple-element.63), channel_id=1, source_target_pairs={{0,24},{1,25},{2,26},{3,27},{4,28},{5,29},{6,30},{7,31},{8,16},{9,... | collective-permute-start | bytes 24584 | tf_op jit(solution)/shard_map/ppermute | solution.py:399
  36.8 3.3 %collective-permute-start.14 = (f32[16,128]{1,0:T(8,128)S(1)}, f32[16,128]{1,0:T(8,128)S(1)}, u32[]{:S(2)}, u32[]{:S(2)}) collective-permute-start(f32[16,128]{1,0:T(8,128)S(1)} %get-tuple-element.62), channel_id=1, source_target_pairs={{0,16},{16,0},{1,17},{17,1},{2,18},{18,2},{3,19},{19,3},{4,20},{20... | collective-permute-start | bytes 24584 | tf_op jit(solution)/shard_map/ppermute | solution.py:362

commit v3 on v2

--- a/solution.py
+++ b/solution.py
@@ -12,7 +12,7 @@
 ROWS = 1024
 LOW = ROWS // 2
 SUB = 8
-STEP = 32
+STEP = 16
 LANES = 128
 MOST_PEERS = 16
 VM = pl.BlockSpec(memory_space=pltpu.VMEM)
@@ -97,7 +97,7 @@
         scratch_shapes=[
             pltpu.VMEM((spd, 2, SUB, width), jnp.bfloat16),
             pltpu.VMEM((1, hot.shape[1]), jnp.int32),
-            pltpu.SemaphoreType.DMA((4,)),
+            pltpu.SemaphoreType.DMA((2,)),
             pltpu.SemaphoreType.DMA((2,)),
         ],
         compiler_params=room(5),
@@ -216,15 +216,15 @@
 
 
 def other_body(spd, places, low_match, high_side, hot_match, total, hot, *refs):
-    chunks, (lower, upper, given) = refs[:-3], refs[-3:]
+    chunks, (out, given) = refs[:-2], refs[-2:]
     pieces = [place + (chunk,) for place, chunk in zip(places, chunks)]
     both, more = partial_sums(spd, pieces, low_match, high_side, hot_match)
     both += total[...]
-    width = lower.shape[1]
+    width = out.shape[1]
     kept, given[...] = split(hot[...] + more)
-    lower[...] = both[:, :width].astype(jnp.bfloat16)
-    upper[pl.ds(0, LOW), :] = both[:, width:].astype(jnp.bfloat16)
-    upper[pl.ds(LOW, kept.shape[0]), :] = kept.astype(jnp.bfloat16)
+    for top in range(2):
+        out[pl.ds(top * LOW, LOW), :] = both[:, top * width:(top + 1) * width].astype(jnp.bfloat16)
+    out[pl.ds(ROWS, kept.shape[0]), :] = kept.astype(jnp.bfloat16)
 
 
 def other_sums(spd, matched, early, items):
@@ -233,12 +233,11 @@
     return pl.pallas_call(
         functools.partial(other_body, spd, places),
         out_shape=(
-            jax.ShapeDtypeStruct((LOW, width), jnp.bfloat16),
-            jax.ShapeDtypeStruct((LOW + half, width), jnp.bfloat16),
+            jax.ShapeDtypeStruct((ROWS + half, width), jnp.bfloat16),
             jax.ShapeDtypeStruct((half, width), jnp.float32),
         ),
         in_specs=[VM] * (5 + len(chunks)),
-        out_specs=(VM,) * 3,
+        out_specs=(VM,) * 2,
         compiler_params=room(8),
         cost_estimate=cost(2 * spd * len(chunks) * width * ROWS, spd * len(chunks) * width * 2),
         name="other_sums",
@@ -290,71 +289,47 @@
     )(block)
 
 
-PIECES = 2
-
-
-def write_rows(top, done, table, far, cold, held, sems):
-    size = LOW // PIECES
+PIECES = 4
+
+
+def last_body(done, matrix, kept, far, same_chip, far_chip, cold, hot, held, sems, hot_held, hot_sem):
+    table = matrix[...]
+    size = ROWS // PIECES
     moves = []
     for piece in range(PIECES):
-        where = pl.ds(top * LOW + piece * size, size)
-        from_far = pl.ds(piece * size, size)
-        held[from_far, :] = done[where, :] + jnp.dot(far[from_far, :], table, preferred_element_type=jnp.float32)
-        moves.append(pltpu.make_async_copy(held.at[from_far], cold.at[where], sems.at[piece]))
+        where = pl.ds(piece * size, size)
+        held[where, :] = done[where, :] + jnp.dot(far[where, :], table, preferred_element_type=jnp.float32)
+        moves.append(pltpu.make_async_copy(held.at[where], cold.at[where], sems.at[piece]))
         moves[-1].start()
-    return moves
-
-
-def lower_body(done, matrix, far, cold, held, sems):
-    for one in write_rows(0, done, matrix[...], far, cold, held, sems):
-        one.wait()
-
-
-def last_scratch(width):
-    return [pltpu.VMEM((LOW, width), jnp.float32), pltpu.SemaphoreType.DMA((PIECES,))]
-
-
-def lower_part(done, matrix, far):
-    width = far.shape[1]
-    return pl.pallas_call(
-        lower_body,
-        out_shape=jax.ShapeDtypeStruct((ROWS, width), jnp.float32),
-        in_specs=[VM] * 3,
-        out_specs=HB,
-        scratch_shapes=last_scratch(width),
-        compiler_params=room(4),
-        cost_estimate=cost(2 * ROWS * width * width, ROWS * width * 5),
-        name="lower_part",
-    )(done, matrix, far)
-
-
-def upper_body(begun, done, matrix, kept, far, same_chip, far_chip, cold, hot, held, sems, hot_held, hot_sem):
-    table = matrix[...]
-    hot_far = far[pl.ds(LOW, hot.shape[0]), :].astype(jnp.float32)
-    hot_held[...] = kept[...] + same_chip[...] + project(hot_far + far_chip[...], table)
-    moves = [pltpu.make_async_copy(hot_held, hot, hot_sem)]
-    moves[0].start()
-    moves += write_rows(1, done, table, far, cold, held, sems)
+        if piece == 0:
+            hot_far = far[pl.ds(ROWS, hot.shape[0]), :].astype(jnp.float32)
+            hot_held[...] = kept[...] + same_chip[...] + project(hot_far + far_chip[...], table)
+            moves.append(pltpu.make_async_copy(hot_held, hot, hot_sem))
+            moves[-1].start()
     for one in moves:
         one.wait()
 
 
-def upper_part(begun, done, matrix, kept, far, same_chip, far_chip):
+def last(done, matrix, kept, far, same_chip, far_chip):
     half, width = same_chip.shape
     return pl.pallas_call(
-        upper_body,
+        last_body,
         out_shape=(
             jax.ShapeDtypeStruct((ROWS, width), jnp.float32),
             jax.ShapeDtypeStruct((half, width), jnp.float32),
         ),
-        in_specs=[HB] + [VM] * 6,
+        in_specs=[VM] * 6,
         out_specs=(HB, HB),
-        scratch_shapes=last_scratch(width) + [pltpu.VMEM((half, width), jnp.float32), pltpu.SemaphoreType.DMA],
-        input_output_aliases={0: 0},
+        scratch_shapes=[
+            pltpu.VMEM((ROWS, width), jnp.float32),
+            pltpu.SemaphoreType.DMA((PIECES,)),
+            pltpu.VMEM((half, width), jnp.float32),
+            pltpu.SemaphoreType.DMA,
+        ],
         compiler_params=room(4),
-        cost_estimate=cost(2 * ROWS * width * width, ROWS * width * 5),
-        name="upper_part",
-    )(begun, done, matrix, kept, far, same_chip, far_chip)
+        cost_estimate=cost(4 * ROWS * width * width, ROWS * width * 10),
+        name="last",
+    )(done, matrix, kept, far, same_chip, far_chip)
 
 
 def swap_reps(block):
@@ -386,11 +361,10 @@
     relayed = send(relay, SUB // 2)
     far_matched = match(far_notes, half_len, hots)
     far_early = early_sums(spd, far_matched, [(shift, 0, got[shift]) for shift in EARLY])
-    lower, upper, far_given = other_sums(
+    partial, far_given = other_sums(
         spd, far_matched, far_early, [(shift, 0, got[shift]) for shift in range(SUB) if shift not in EARLY]
     )
-    far_lower = send(lower, SUB)
-    far_upper = send(upper, SUB)
+    far = send(partial, SUB)
     own = [(shift, spd, got[shift]) for shift in (0,) + PLANE if shift not in SPLIT]
     own += [(shift, 0, send(block, shift)) for shift, block in zip(SPLIT, blocks[SUB:])]
     own += [(SUB // 2, 0, relayed)]
@@ -407,8 +381,7 @@
         spd, own_matched, own_early, [(SUB // 2 + shift, 0, one) for shift, one in zip(PLANE, second)], matrix
     )
     same_chip = swap_reps(given)
-    begun = lower_part(done, matrix, far_lower)
-    cold, hot = upper_part(begun, done, matrix, kept, far_upper, same_chip, far_chip)
+    cold, hot = last(done, matrix, kept, far, same_chip, far_chip)
     return cold[None, None], hot[None]
 
 

time: 41.5 us -> 38.4 us (0.925)
  the two profiles are of different devices: /device:TPU:9 before, /device:TPU:0 now
where the time goes in v3:
time: 38.4 us; the launch traced here: 38.3 us
  starting transfers between devices  21.7 us (57%)
  waiting for transfers between devices  8.36 us (22%)
  Pallas kernels  7.4 us (19%)
  between operations  0.78 us (2%)
    ppermute x13, starting transfers between devices, send(): return lax.ppermute(block, 'tab', [(i, i ^ shift) for i in range(count)])  21.6 us
    ppermute x13, waiting for transfers between devices, send(): return lax.ppermute(block, 'tab', [(i, i ^ shift) for i in range(count)])  7.21 us
    pallas_call x2, Pallas kernels, early_sums(): pl.pallas_call(functools.partial(own_early_body if own else early_body, s...  1.97 us
    pallas_call x2, Pallas kernels, match(): pl.pallas_call(fill_match, out_shape=(jax.ShapeDtypeStruct((LOW, total),...  1.83 us
    pallas_call x1, Pallas kernels, prep(): pl.pallas_call(prep_body, out_shape=(jax.ShapeDtypeStruct((1, lookups.sha...  1.69 us
    ppermute x1, waiting for transfers between devices, swap_reps(): return lax.ppermute(block, 'rep', [(r, r ^ 1) for r in range(reps)])  1.15 us
    pallas_call x1, Pallas kernels, last(): pl.pallas_call(last_body, out_shape=(jax.ShapeDtypeStruct((ROWS, width),...  0.99 us
  transfers between devices with their start and end apart: 15, of which 4 were waited for; matrix products, arithmetic and copies ran while one was open for 0% of the time, Pallas kernels for 12%

profile of v3, /device:TPU:0, one launch (start us, length us, event | category | flops | bytes accessed | tf_op | source)
XLA Modules:
  0.0 38.3 jit_solution(900380033318471947)
XLA Ops:
  0.6 1.7 %prep.1 = (s32[1,4224]{1,0:T(1,128)S(1)}, bf16[512,128]{1,0:T(8,128)(2,1)S(1)}, bf16[512,128]{1,0:T(8,128)(2,1)S(1)}, bf16[512,128]{1,0:T(8,128)(2,1)S(1)}, bf16...) custom-call(bf16[256,2,8,128]{3,2,1,0:T(8,128)(2,1)} %bitcast.5, ...), custom_call_target="tpu_custom_call" | custom-call | flops 268435456 | bytes 2097152 | tf_op jit(solution)/shard_map/prep/pallas_call | solution.py:89
  2.3 4.1 %collective-permute-start.10 = (bf16[256,128]{1,0:T(8,128)(2,1)S(1)}, bf16[256,128]{1,0:T(8,128)(2,1)S(1)}, u32[]{:S(2)}, u32[]{:S(2)}) collective-permute-start(bf16[256,128]{1,0:T(8,128)(2,1)S(1)} %get-tuple-element.55), channel_id=1, source_target_pairs={{0,6},{1,7},{2,4},{3,5},{4,2},{5,3},{6,0},{7,1},{8,14},{9,15},{10,... | collective-permute-start | bytes 196616 | tf_op jit(solution)/shard_map/ppermute | solution.py:354
  6.4 1.4 %collective-permute-start.11 = (bf16[256,128]{1,0:T(8,128)(2,1)S(1)}, bf16[256,128]{1,0:T(8,128)(2,1)S(1)}, u32[]{:S(2)}, u32[]{:S(2)}) collective-permute-start(bf16[256,128]{1,0:T(8,128)(2,1)S(1)} %get-tuple-element.56), channel_id=1, source_target_pairs={{0,5},{1,4},{2,7},{3,6},{4,1},{5,0},{6,3},{7,2},{8,13},{9,12},{10,... | collective-permute-start | bytes 196616 | tf_op jit(solution)/shard_map/ppermute | solution.py:354
  7.8 0.2 collective-permute-start.2
  7.9 2.9 %collective-permute-start.7 = (s32[1,4224]{1,0:T(1,128)S(1)}, s32[1,4224]{1,0:T(1,128)S(1)}, u32[]{:S(2)}, u32[]{:S(2)}) collective-permute-start(s32[1,4224]{1,0:T(1,128)S(1)} %get-tuple-element.33.notes), channel_id=1, source_target_pairs={{0,8},{1,9},{2,10},{3,11},{4,12},{5,13},{6,14},{7,15},{8,0},{9,1},... | collective-permute-start | bytes 50696 | tf_op jit(solution)/shard_map/ppermute | solution.py:354
  10.8 1.6 %collective-permute-start.8 = (bf16[256,128]{1,0:T(8,128)(2,1)S(1)}, bf16[256,128]{1,0:T(8,128)(2,1)S(1)}, u32[]{:S(2)}, u32[]{:S(2)}) collective-permute-start(bf16[256,128]{1,0:T(8,128)(2,1)S(1)} %get-tuple-element.53), channel_id=1, source_target_pairs={{0,4},{1,5},{2,6},{3,7},{4,0},{5,1},{6,2},{7,3},{8,12},{9,13},{10,... | collective-permute-start | bytes 196616 | tf_op jit(solution)/shard_map/ppermute | solution.py:354
  12.4 0.3 collective-permute-done.7.notes
  12.7 1.8 %collective-permute-start = (bf16[512,128]{1,0:T(8,128)(2,1)S(1)}, bf16[512,128]{1,0:T(8,128)(2,1)S(1)}, u32[]{:S(2)}, u32[]{:S(2)}) collective-permute-start(bf16[512,128]{1,0:T(8,128)(2,1)S(1)} %get-tuple-element.38), channel_id=1, source_target_pairs={{0,1},{1,0},{2,3},{3,2},{4,5},{5,4},{6,7},{7,6},{8,9},{9,8},{10,11... | collective-permute-start | bytes 393224 | tf_op jit(solution)/shard_map/ppermute | solution.py:354
  14.5 1.5 %collective-permute-start.1 = (bf16[512,128]{1,0:T(8,128)(2,1)S(1)}, bf16[512,128]{1,0:T(8,128)(2,1)S(1)}, u32[]{:S(2)}, u32[]{:S(2)}) collective-permute-start(bf16[512,128]{1,0:T(8,128)(2,1)S(1)} %get-tuple-element.39), channel_id=1, source_target_pairs={{0,2},{1,3},{2,0},{3,1},{4,6},{5,7},{6,4},{7,5},{8,10},{9,11},{10,... | collective-permute-start | bytes 393224 | tf_op jit(solution)/shard_map/ppermute | solution.py:354
  16.0 1.4 %collective-permute-start.9 = (bf16[256,128]{1,0:T(8,128)(2,1)S(1)}, bf16[256,128]{1,0:T(8,128)(2,1)S(1)}, u32[]{:S(2)}, u32[]{:S(2)}) collective-permute-start(bf16[256,128]{1,0:T(8,128)(2,1)S(1)} %get-tuple-element.54), channel_id=1, source_target_pairs={{0,7},{1,6},{2,5},{3,4},{4,3},{5,2},{6,1},{7,0},{8,15},{9,14},{10,... | collective-permute-start | bytes 196616 | tf_op jit(solution)/shard_map/ppermute | solution.py:354
  17.5 0.2 collective-permute-start.3
  17.7 0.9 %shard_map.69 = (bf16[512,2048]{1,0:T(8,128)(2,1)S(1)}, bf16[2048,128]{1,0:T(8,128)(2,1)S(1)}, bf16[32,2048]{1,0:T(8,128)(2,1)S(1)}) custom-call(s32[1,4224]{1,0:T(1,128)S(1)} %collective-permute-done.7.notes), custom_call_target="tpu_custom_call" | custom-call | flops 419430400 | bytes 2097152 | tf_op jit(solution)/shard_map/pallas_call | solution.py:134
  18.6 4.1 %collective-permute-done.9.refs_3_ = bf16[256,128]{1,0:T(8,128)(2,1)S(1)} collective-permute-done((bf16[256,128]{1,0:T(8,128)(2,1)S(1)}, bf16[256,128]{1,0:T(8,128)(2,1)S(1)}, u32[]{:S(2)}, u32[]{:S(2)}) %collective-permute-start.9) | collective-permute-done | bytes 65568 | tf_op jit(solution)/shard_map/ppermute | solution.py:354
  22.7 0.6 %far_early.1 = (f32[512,256]{1,0:T(8,128)S(1)}, f32[32,128]{1,0:T(8,128)S(1)}) custom-call(bf16[512,2048]{1,0:T(8,128)(2,1)S(1)} %get-tuple-element.50.low_match, bf16[2048,128]{1,0:T(8,128)(2,1)S(1)} %get-tuple-element.51.high_side, bf16[32,2048]{1,0:T(8,128)(2,1)S(1)} %get-tuple-element.52.hot_match, bf16[512,128]{1,0:T(8,128)(2,1)S(1)} %get-tuple-element.37.refs_0_, ...), custom_call_target="tpu_custom_call" | custom-call | flops 402653184 | bytes 393216 | tf_op jit(solution)/shard_map/far_early/pallas_call | solution.py:207
  23.4 0.3 other_sums.1
  23.8 2.7 %collective-permute-start.12 = (bf16[1040,128]{1,0:T(8,128)(2,1)S(1)}, bf16[1040,128]{1,0:T(8,128)(2,1)S(1)}, u32[]{:S(2)}, u32[]{:S(2)}) collective-permute-start(bf16[1040,128]{1,0:T(8,128)(2,1)S(1)} %get-tuple-element.59), channel_id=1, source_target_pairs={{0,8},{1,9},{2,10},{3,11},{4,12},{5,13},{6,14},{7,15},{8,0},{9,1},... | collective-permute-start | bytes 798728 | tf_op jit(solution)/shard_map/ppermute | solution.py:354
  26.4 1.5 %collective-permute-start.4 = (bf16[256,128]{1,0:T(8,128)(2,1)S(1)}, bf16[256,128]{1,0:T(8,128)(2,1)S(1)}, u32[]{:S(2)}, u32[]{:S(2)}) collective-permute-start(bf16[256,128]{1,0:T(8,128)(2,1)S(1)} %get-tuple-element.45), channel_id=1, source_target_pairs={{0,1},{1,0},{2,3},{3,2},{4,5},{5,4},{6,7},{7,6},{8,9},{9,8},{10,11... | collective-permute-start | bytes 196616 | tf_op jit(solution)/shard_map/ppermute | solution.py:354
  27.9 2.4 %collective-permute-start.5 = (bf16[256,128]{1,0:T(8,128)(2,1)S(1)}, bf16[256,128]{1,0:T(8,128)(2,1)S(1)}, u32[]{:S(2)}, u32[]{:S(2)}) collective-permute-start(bf16[256,128]{1,0:T(8,128)(2,1)S(1)} %get-tuple-element.46), channel_id=1, source_target_pairs={{0,2},{1,3},{2,0},{3,1},{4,6},{5,7},{6,4},{7,5},{8,10},{9,11},{10,... | collective-permute-start | bytes 196616 | tf_op jit(solution)/shard_map/ppermute | solution.py:354
  30.3 0.9 %shard_map.68 = (bf16[512,2048]{1,0:T(8,128)(2,1)S(1)}, bf16[2048,128]{1,0:T(8,128)(2,1)S(1)}, bf16[32,2048]{1,0:T(8,128)(2,1)S(1)}) custom-call(s32[1,4224]{1,0:T(1,128)S(1)} %get-tuple-element.33.notes), custom_call_target="tpu_custom_call" | custom-call | flops 419430400 | bytes 2097152 | tf_op jit(solution)/shard_map/pallas_call | solution.py:134
  31.3 1.3 %own_early.1 = (f32[512,256]{1,0:T(8,128)S(1)}, f32[32,128]{1,0:T(8,128)S(1)}, bf16[128,128]{1,0:T(8,128)(2,1)S(1)}) custom-call(s32[16]{0:T(128)S(1)} %copy-done.1, bf16[128,128]{1,0:T(8,128)(2,1)S(1)} %bitcast.4, bf16[512,2048]{1,0:T(8,128)(2,1)S(1)} %get-tuple-element.34.low_match, bf16[2048,128]{1,0:T(8,128)(2,1)S(1)} %get-tuple-element.35.high_side, ...), custom_call_target="tpu_custom_call" | custom-call | flops 335544320 | bytes 327680 | tf_op jit(solution)/shard_map/own_early/pallas_call | solution.py:207
  32.7 2.8 %collective-permute-done.6.refs_2_ = bf16[256,128]{1,0:T(8,128)(2,1)S(1)} collective-permute-done((bf16[256,128]{1,0:T(8,128)(2,1)S(1)}, bf16[256,128]{1,0:T(8,128)(2,1)S(1)}, u32[]{:S(2)}, u32[]{:S(2)}) %collective-permute-start.6) | collective-permute-done | bytes 65568 | tf_op jit(solution)/shard_map/ppermute | solution.py:354
  35.5 0.6 %own_sums.1 = (f32[1024,128]{1,0:T(8,128)S(1)}, f32[16,128]{1,0:T(8,128)S(1)}, f32[16,128]{1,0:T(8,128)S(1)}) custom-call(bf16[128,128]{1,0:T(8,128)(2,1)S(1)} %get-tuple-element.42.matrix, bf16[512,2048]{1,0:T(8,128)(2,1)S(1)} %get-tuple-element.34.low_match, bf16[2048,128]{1,0:T(8,128)(2,1)S(1)} %get-tuple-element.35.high_side, ...), custom_call_target="tpu_custom_call" | custom-call | flops 201326592 | bytes 196608 | tf_op jit(solution)/shard_map/own_sums/pallas_call | solution.py:262
  36.1 1.1 %collective-permute-done.13.same_chip = f32[16,128]{1,0:T(8,128)S(1)} collective-permute-done((f32[16,128]{1,0:T(8,128)S(1)}, f32[16,128]{1,0:T(8,128)S(1)}, u32[]{:S(2)}, u32[]{:S(2)}) %collective-permute-start.13) | collective-permute-done | bytes 8224 | tf_op jit(solution)/shard_map/ppermute | solution.py:337
  37.3 1.0 %last.1 = (f32[1024,128]{1,0:T(8,128)}, f32[16,128]{1,0:T(8,128)}) custom-call(f32[1024,128]{1,0:T(8,128)S(1)} %get-tuple-element.48.done, bf16[128,128]{1,0:T(8,128)(2,1)S(1)} %get-tuple-element.42.matrix, f32[16,128]{1,0:T(8,128)S(1)} %get-tuple-element.49.kept, bf16[1040,128]{1,0:T(8,128)(2,1)S(1)} %collective-permute-done.12.far, ...), custom_call_target="tpu_custom_call" | custom-call | flops 67108864 | bytes 1310720 | tf_op jit(solution)/shard_map/last/pallas_call | solution.py:315
  (19 shorter events, 0.2 us)
Async XLA Ops:
  2.3 12.2 %collective-permute-start.10 = (bf16[256,128]{1,0:T(8,128)(2,1)S(1)}, bf16[256,128]{1,0:T(8,128)(2,1)S(1)}, u32[]{:S(2)}, u32[]{:S(2)}) collective-permute-start(bf16[256,128]{1,0:T(8,128)(2,1)S(1)} %get-tuple-element.55), channel_id=1, source_target_pairs={{0,6},{1,7},{2,4},{3,5},{4,2},{5,3},{6,0},{7,1},{8,14},{9,15},{10,... | collective-permute-start | bytes 196616 | tf_op jit(solution)/shard_map/ppermute | solution.py:354
  6.4 9.6 %collective-permute-start.11 = (bf16[256,128]{1,0:T(8,128)(2,1)S(1)}, bf16[256,128]{1,0:T(8,128)(2,1)S(1)}, u32[]{:S(2)}, u32[]{:S(2)}) collective-permute-start(bf16[256,128]{1,0:T(8,128)(2,1)S(1)} %get-tuple-element.56), channel_id=1, source_target_pairs={{0,5},{1,4},{2,7},{3,6},{4,1},{5,0},{6,3},{7,2},{8,13},{9,12},{10,... | collective-permute-start | bytes 196616 | tf_op jit(solution)/shard_map/ppermute | solution.py:354
  7.8 14.9 %collective-permute-start.2 = (bf16[512,128]{1,0:T(8,128)(2,1)S(1)}, bf16[512,128]{1,0:T(8,128)(2,1)S(1)}, u32[]{:S(2)}, u32[]{:S(2)}) collective-permute-start(bf16[512,128]{1,0:T(8,128)(2,1)S(1)} %get-tuple-element.40), channel_id=1, source_target_pairs={{0,3},{1,2},{2,1},{3,0},{4,7},{5,6},{6,5},{7,4},{8,11},{9,10},{10,... | collective-permute-start | bytes 393224 | tf_op jit(solution)/shard_map/ppermute | solution.py:354
  7.9 4.7 %collective-permute-start.7 = (s32[1,4224]{1,0:T(1,128)S(1)}, s32[1,4224]{1,0:T(1,128)S(1)}, u32[]{:S(2)}, u32[]{:S(2)}) collective-permute-start(s32[1,4224]{1,0:T(1,128)S(1)} %get-tuple-element.33.notes), channel_id=1, source_target_pairs={{0,8},{1,9},{2,10},{3,11},{4,12},{5,13},{6,14},{7,15},{8,0},{9,1},... | collective-permute-start | bytes 50696 | tf_op jit(solution)/shard_map/ppermute | solution.py:354
  10.8 6.6 %collective-permute-start.8 = (bf16[256,128]{1,0:T(8,128)(2,1)S(1)}, bf16[256,128]{1,0:T(8,128)(2,1)S(1)}, u32[]{:S(2)}, u32[]{:S(2)}) collective-permute-start(bf16[256,128]{1,0:T(8,128)(2,1)S(1)} %get-tuple-element.53), channel_id=1, source_target_pairs={{0,4},{1,5},{2,6},{3,7},{4,0},{5,1},{6,2},{7,3},{8,12},{9,13},{10,... | collective-permute-start | bytes 196616 | tf_op jit(solution)/shard_map/ppermute | solution.py:354
  12.7 10.7 %collective-permute-start = (bf16[512,128]{1,0:T(8,128)(2,1)S(1)}, bf16[512,128]{1,0:T(8,128)(2,1)S(1)}, u32[]{:S(2)}, u32[]{:S(2)}) collective-permute-start(bf16[512,128]{1,0:T(8,128)(2,1)S(1)} %get-tuple-element.38), channel_id=1, source_target_pairs={{0,1},{1,0},{2,3},{3,2},{4,5},{5,4},{6,7},{7,6},{8,9},{9,8},{10,11... | collective-permute-start | bytes 393224 | tf_op jit(solution)/shard_map/ppermute | solution.py:354
  14.5 8.9 %collective-permute-start.1 = (bf16[512,128]{1,0:T(8,128)(2,1)S(1)}, bf16[512,128]{1,0:T(8,128)(2,1)S(1)}, u32[]{:S(2)}, u32[]{:S(2)}) collective-permute-start(bf16[512,128]{1,0:T(8,128)(2,1)S(1)} %get-tuple-element.39), channel_id=1, source_target_pairs={{0,2},{1,3},{2,0},{3,1},{4,6},{5,7},{6,4},{7,5},{8,10},{9,11},{10,... | collective-permute-start | bytes 393224 | tf_op jit(solution)/shard_map/ppermute | solution.py:354
  16.0 6.7 %collective-permute-start.9 = (bf16[256,128]{1,0:T(8,128)(2,1)S(1)}, bf16[256,128]{1,0:T(8,128)(2,1)S(1)}, u32[]{:S(2)}, u32[]{:S(2)}) collective-permute-start(bf16[256,128]{1,0:T(8,128)(2,1)S(1)} %get-tuple-element.54), channel_id=1, source_target_pairs={{0,7},{1,6},{2,5},{3,4},{4,3},{5,2},{6,1},{7,0},{8,15},{9,14},{10,... | collective-permute-start | bytes 196616 | tf_op jit(solution)/shard_map/ppermute | solution.py:354
  17.5 8.9 %collective-permute-start.3 = (bf16[1024,128]{1,0:T(8,128)(2,1)S(1)}, bf16[1024,128]{1,0:T(8,128)(2,1)S(1)}, u32[]{:S(2)}, u32[]{:S(2)}) collective-permute-start(bf16[1024,128]{1,0:T(8,128)(2,1)S(1)} %get-tuple-element.41), channel_id=1, source_target_pairs={{0,4},{1,5},{2,6},{3,7},{4,0},{5,1},{6,2},{7,3},{8,12},{9,13},{10,... | collective-permute-start | bytes 786440 | tf_op jit(solution)/shard_map/ppermute | solution.py:354
  23.4 7.9 %copy-start = (bf16[1,128,128]{2,1,0:T(8,128)(2,1)S(1)}, bf16[1,128,128]{2,1,0:T(8,128)(2,1)}, u32[]{:S(2)}) copy-start(bf16[1,128,128]{2,1,0:T(8,128)(2,1)} %param.7) | copy-start | bytes 98308
  23.4 7.9 %copy-start.1 = (s32[16]{0:T(128)S(1)}, s32[16]{0:T(128)}, u32[]{:S(2)}) copy-start(s32[16]{0:T(128)} %widths.1) | copy-start | bytes 196
  23.8 13.5 %collective-permute-start.12 = (bf16[1040,128]{1,0:T(8,128)(2,1)S(1)}, bf16[1040,128]{1,0:T(8,128)(2,1)S(1)}, u32[]{:S(2)}, u32[]{:S(2)}) collective-permute-start(bf16[1040,128]{1,0:T(8,128)(2,1)S(1)} %get-tuple-element.59), channel_id=1, source_target_pairs={{0,8},{1,9},{2,10},{3,11},{4,12},{5,13},{6,14},{7,15},{8,0},{9,1},... | collective-permute-start | bytes 798728 | tf_op jit(solution)/shard_map/ppermute | solution.py:354
  26.4 6.2 %collective-permute-start.4 = (bf16[256,128]{1,0:T(8,128)(2,1)S(1)}, bf16[256,128]{1,0:T(8,128)(2,1)S(1)}, u32[]{:S(2)}, u32[]{:S(2)}) collective-permute-start(bf16[256,128]{1,0:T(8,128)(2,1)S(1)} %get-tuple-element.45), channel_id=1, source_target_pairs={{0,1},{1,0},{2,3},{3,2},{4,5},{5,4},{6,7},{7,6},{8,9},{9,8},{10,11... | collective-permute-start | bytes 196616 | tf_op jit(solution)/shard_map/ppermute | solution.py:354
  27.9 4.7 %collective-permute-start.5 = (bf16[256,128]{1,0:T(8,128)(2,1)S(1)}, bf16[256,128]{1,0:T(8,128)(2,1)S(1)}, u32[]{:S(2)}, u32[]{:S(2)}) collective-permute-start(bf16[256,128]{1,0:T(8,128)(2,1)S(1)} %get-tuple-element.46), channel_id=1, source_target_pairs={{0,2},{1,3},{2,0},{3,1},{4,6},{5,7},{6,4},{7,5},{8,10},{9,11},{10,... | collective-permute-start | bytes 196616 | tf_op jit(solution)/shard_map/ppermute | solution.py:354
  30.3 5.2 %collective-permute-start.6 = (bf16[256,128]{1,0:T(8,128)(2,1)S(1)}, bf16[256,128]{1,0:T(8,128)(2,1)S(1)}, u32[]{:S(2)}, u32[]{:S(2)}) collective-permute-start(bf16[256,128]{1,0:T(8,128)(2,1)S(1)} %get-tuple-element.47), channel_id=1, source_target_pairs={{0,3},{1,2},{2,1},{3,0},{4,7},{5,6},{6,5},{7,4},{8,11},{9,10},{10,... | collective-permute-start | bytes 196616 | tf_op jit(solution)/shard_map/ppermute | solution.py:354
  31.2 4.9 %collective-permute-start.14 = (f32[16,128]{1,0:T(8,128)S(1)}, f32[16,128]{1,0:T(8,128)S(1)}, u32[]{:S(2)}, u32[]{:S(2)}) collective-permute-start(f32[16,128]{1,0:T(8,128)S(1)} %get-tuple-element.61), channel_id=1, source_target_pairs={{0,24},{1,25},{2,26},{3,27},{4,28},{5,29},{6,30},{7,31},{8,16},{9,... | collective-permute-start | bytes 24584 | tf_op jit(solution)/shard_map/ppermute | solution.py:373
  36.0 1.2 %collective-permute-start.13 = (f32[16,128]{1,0:T(8,128)S(1)}, f32[16,128]{1,0:T(8,128)S(1)}, u32[]{:S(2)}, u32[]{:S(2)}) collective-permute-start(f32[16,128]{1,0:T(8,128)S(1)} %get-tuple-element.60), channel_id=1, source_target_pairs={{0,16},{16,0},{1,17},{17,1},{2,18},{18,2},{3,19},{19,3},{4,20},{20... | collective-permute-start | bytes 24584 | tf_op jit(solution)/shard_map/ppermute | solution.py:337
